TPU v7x, 512 devices: a whole 4x8x8 slice. The times are simulated.
512 devices in a mesh: grp: 8 (over x, core), sub: 64 (over z, y).
Axes of the slice: x: 4, y: 8, z: 8, core: 2. Of those that a mesh axis runs over, the one named last changes fastest.
Arguments:
- overall_quantity_unnormalized: float32 [16, 64, 1024, 128], P(None, 'grp', 'sub'), may hold values from 0.05 to 1
- reservoir_pressure_field: float32 [64, 1024, 128], P('grp', 'sub'), may hold values from 0.7 to 1.3
- reservoir_heat_level: float32 [64, 1024, 128], P('grp', 'sub'), may hold values from 0.9 to 1.2
- condensed_flag: int32 [64, 1024, 128], P('grp', 'sub'), may hold values 0 or 1
- permeability_field: float32 [64, 1024, 128], P('grp', 'sub'), may hold values from 0.1 to 10
- pore_capacity: float32 [64, 1024, 128], P('grp', 'sub'), may hold values from 0.05 to 0.3
- former_chemical_quantity: float32 [16, 64, 1024, 128], P(None, 'grp', 'sub'), may hold values from 0 to 0.03
- transmissibility_multipliers: float32 [3], replicated, may hold values from 0.3 to 3
- viscosity_pair: float32 [2], replicated, may hold values from 0.3 to 3
- crit_kelvin_values: float32 [16], replicated, may hold values from 0.3 to 2.5
- attraction_parameters: float32 [16], replicated, may hold values from 0.3 to 4
- repulsive_parameters: float32 [16], replicated, may hold values from 0.02 to 0.15
- attraction_thermal_gradients: float32 [16], replicated, may hold values from 0.3 to 1.2
- binary_coupling_matrix: float32 [16, 16], replicated, may hold values from 0 to 0.3, as said below
- injected_recipe_unnormalized: float32 [16], replicated, may hold values from 0.05 to 1
- perforated_locale: int32 [131072], P(('grp', 'sub')), may hold values from 0 to 16383
- perforated_member: int32 [131072, 1], P(('grp', 'sub')), may hold values from 0 to 63; in each aligned block of 256 rows (0 to 255, 256 to 511, ...) at most 10 rows name the same one
- connection_conduit_piece: int32 [131072], P(('grp', 'sub')), may hold values from 0 to 31
- connection_inflow_strength: float32 [131072], P(('grp', 'sub')), may hold values from 0.02 to 0.2
- group_member_place: int32 [8, 64], P('grp'), may hold values from 0 to 63, each once within a row
- conduit_pieces_toe_forward: int32 [512, 32], P(('grp', 'sub')), may hold values from 0 to 31, each once within a row
- conduit_piece_pressures: float32 [512, 32], P(('grp', 'sub')), may hold values from 0.7 to 1.3
- downstream_exit_pressure: float32 [512], P(('grp', 'sub')), may hold values from 0.6 to 1.2
- friction_factors: float32 [512], P(('grp', 'sub')), may hold values from 3.0517578e-05 to 0.00030517578
Outputs:
- residual: float32 [16, 64, 1024, 128], P(None, 'grp', 'sub')
- ln_phi: bfloat16 [16, 64, 1024, 128], P(None, 'grp', 'sub')
- well_residual: float32 [512, 32], P(('grp', 'sub'))
Inputs may be any that keep to these rules, and one draw needn't show every extreme that they name: `perforated_locale`: flattened index (first, second, layer) of a cell of the listing device's own block. `perforated_member`: a well of the listing device's group; among the 256 rows of one device at most 10 name the same well. `group_member_place`: each row is a permutation; slot j of a group lies on the group's device j. `conduit_pieces_toe_forward`: each row is a permutation of the segments. `binary_coupling_matrix`: symmetric with zero diagonal.
All inputs are finite; a program needn't handle non-finite values. No bound on the sum of `condensed_flag` on one device may be relied on, other than what follows from the above.
Results may differ from a plain program's by a relative error of at most 0.001.
Values sent between devices are 32-bit elements; how exact they have to be, the bound alone decides.
A program may use at most 64 MiB of HBM per device.

v0:
```python
import math

import jax
import jax.numpy as jnp
from jax import lax
from jax.sharding import PartitionSpec as P

NEWT = 8


ROOT_TWO = math.sqrt(2.0)


def padded_2(array, sides, width):
    edges = {}
    for axis, dim in sides:
        size, length = (lax.axis_size(axis), array.shape[dim])
        up = [(i, (i + 1) % size) for i in range(size - 1)]
        last = lax.slice_in_dim(array, length - width, length, axis=dim)
        initial = lax.slice_in_dim(array, 0, width, axis=dim)
        edges[dim] = (
            lax.ppermute(last, axis, up),
            lax.ppermute(initial, axis, [(b, a) for a, b in up]),
        )
    done = []
    for _, dim in sides:
        low, high = edges[dim]
        around = [(width, width) if d in done else (0, 0) for d in range(array.ndim)]
        array = jnp.concatenate([jnp.pad(low, around), array, jnp.pad(high, around)], axis=dim)
        done.append(dim)
    return array


def in_order(pieces, dim):
    shape = list(pieces.shape[1:])
    shape[dim] *= pieces.shape[0]
    return jnp.moveaxis(pieces, 0, dim).reshape(shape)


def from_everyone(array, axis):
    size = lax.axis_size(axis)
    return lax.all_to_all(
        jnp.broadcast_to(array[None], (size, *array.shape)), axis, 0, 0, tiled=True
    )


def gathered_copies(array, axis, dim):
    return in_order(from_everyone(array, axis), dim)


def cut_along(array, dim, size):
    before, after = (array.shape[:dim], array.shape[dim + 1 :])
    return jnp.moveaxis(array.reshape(*before, size, -1, *after), dim, 0)


def summed_on_arrival(array, axis, dim):
    pieces = cut_along(array, dim, lax.axis_size(axis))
    arrived = lax.all_to_all(pieces, axis, split_axis=0, concat_axis=0, tiled=True)
    return arrived.sum(axis=0)


def gas_oil_partition(
    overall_quantity_unnormalized,
    reservoir_pressure_field,
    reservoir_heat_level,
    condensed_flag,
    crit_kelvin_values,
    attraction_parameters,
    repulsive_parameters,
    attraction_thermal_gradients,
    binary_coupling_matrix,
    viscosity_pair,
):
    shape = overall_quantity_unnormalized.shape
    replicate_across = (slice(None),) + (None,) * (len(shape) - 1)
    chemical_labels = overall_quantity_unnormalized / jnp.sum(overall_quantity_unnormalized, axis=0)
    thermal_adjuster = (
        1.0
        + attraction_thermal_gradients[replicate_across]
        * (1.0 - jnp.sqrt(reservoir_heat_level / crit_kelvin_values[replicate_across]))
    ) ** 2
    blended_attraction = (
        attraction_parameters[replicate_across]
        * thermal_adjuster
        * reservoir_pressure_field
        / (reservoir_heat_level * reservoir_heat_level)
    )
    roots = jnp.sqrt(blended_attraction)
    mixture_excluded_volume = (
        repulsive_parameters[replicate_across] * reservoir_pressure_field / reservoir_heat_level
    )
    mixed = jnp.dot(
        1.0 - binary_coupling_matrix,
        (roots * chemical_labels).reshape(shape[0], -1),
        precision=lax.Precision.HIGHEST,
    ).reshape(shape)
    psi = roots * mixed
    big_a = jnp.sum(chemical_labels * psi, axis=0)
    big_b = jnp.sum(chemical_labels * mixture_excluded_volume, axis=0)
    deviation_zvalue = jnp.where(condensed_flag == 1, big_b + 0.01, 1.0 + big_b)
    lin_c2 = big_b - 1.0
    lin_c1 = big_a - 3.0 * big_b * big_b - 2.0 * big_b
    lin_c0 = big_b * big_b + big_b * big_b * big_b - big_a * big_b
    for step in range(NEWT):
        value = (
            (deviation_zvalue + lin_c2) * deviation_zvalue + lin_c1
        ) * deviation_zvalue + lin_c0
        slope = (3.0 * deviation_zvalue + 2.0 * lin_c2) * deviation_zvalue + lin_c1
        deviation_zvalue = jnp.maximum(
            deviation_zvalue - value / jnp.maximum(slope, 0.1), big_b + 0.01
        )
    ratio = jnp.log(
        (deviation_zvalue + (1.0 + ROOT_TWO) * big_b)
        / (deviation_zvalue + (1.0 - ROOT_TWO) * big_b)
    )
    natural_log_activity = (
        mixture_excluded_volume / big_b * (deviation_zvalue - 1.0)
        - jnp.log(deviation_zvalue - big_b)
        - (
            psi / (ROOT_TWO * big_b)
            - big_a * mixture_excluded_volume / (2.0 * ROOT_TWO * big_b * big_b)
        )
        * ratio
    )
    blended_dilution_ratio = reservoir_pressure_field / (deviation_zvalue * reservoir_heat_level)
    visc = jnp.where(condensed_flag == 1, viscosity_pair[1], viscosity_pair[0])
    relative_flow_ease = blended_dilution_ratio / visc
    return (chemical_labels, natural_log_activity, blended_dilution_ratio, relative_flow_ease)


def face(c_a, p_a, k_a, c_b, p_b, k_b, factor):
    trans = factor * 2.0 * k_a * k_b / (k_a + k_b)
    return trans * (p_a - p_b) * jnp.where(p_a > p_b, c_a, c_b)


def layer_shift(arr, upward):
    width = [(0, 0)] * (arr.ndim - 1) + [(1, 1)]
    padded = jnp.pad(arr, width)
    if upward:
        return padded[..., 2:]
    return padded[..., :-2]


def all_fluxes(storage_term, carried_pad, press_pad, perm_pad, transmissibility_multipliers):
    c_a = carried_pad[:, 1:-1, 1:-1]
    p_a = press_pad[1:-1, 1:-1]
    k_a = perm_pad[1:-1, 1:-1]
    total = storage_term
    total = total + face(
        c_a,
        p_a,
        k_a,
        carried_pad[:, 2:, 1:-1],
        press_pad[2:, 1:-1],
        perm_pad[2:, 1:-1],
        transmissibility_multipliers[0],
    )
    total = total + face(
        c_a,
        p_a,
        k_a,
        carried_pad[:, :-2, 1:-1],
        press_pad[:-2, 1:-1],
        perm_pad[:-2, 1:-1],
        transmissibility_multipliers[0],
    )
    total = total + face(
        c_a,
        p_a,
        k_a,
        carried_pad[:, 1:-1, 2:],
        press_pad[1:-1, 2:],
        perm_pad[1:-1, 2:],
        transmissibility_multipliers[1],
    )
    total = total + face(
        c_a,
        p_a,
        k_a,
        carried_pad[:, 1:-1, :-2],
        press_pad[1:-1, :-2],
        perm_pad[1:-1, :-2],
        transmissibility_multipliers[1],
    )
    total = total + face(
        c_a,
        p_a,
        k_a,
        layer_shift(c_a, True),
        layer_shift(p_a, True),
        layer_shift(k_a, True),
        transmissibility_multipliers[2],
    )
    total = total + face(
        c_a,
        p_a,
        k_a,
        layer_shift(c_a, False),
        layer_shift(p_a, False),
        layer_shift(k_a, False),
        transmissibility_multipliers[2],
    )
    return total


def per_device(
    overall_quantity_unnormalized,
    reservoir_pressure_field,
    reservoir_heat_level,
    condensed_flag,
    permeability_field,
    pore_capacity,
    former_chemical_quantity,
    transmissibility_multipliers,
    viscosity_pair,
    crit_kelvin_values,
    attraction_parameters,
    repulsive_parameters,
    attraction_thermal_gradients,
    binary_coupling_matrix,
    injected_recipe_unnormalized,
    perforated_locale,
    perforated_member,
    connection_conduit_piece,
    connection_inflow_strength,
    group_member_place,
    conduit_pieces_toe_forward,
    conduit_piece_pressures,
    downstream_exit_pressure,
    friction_factors,
):
    ncomp = overall_quantity_unnormalized.shape[0]
    chemical_labels, natural_log_activity, blended_dilution_ratio, relative_flow_ease = (
        gas_oil_partition(
            overall_quantity_unnormalized,
            reservoir_pressure_field,
            reservoir_heat_level,
            condensed_flag,
            crit_kelvin_values,
            attraction_parameters,
            repulsive_parameters,
            attraction_thermal_gradients,
            binary_coupling_matrix,
            viscosity_pair,
        )
    )
    state = jnp.concatenate(
        [
            relative_flow_ease[None] * chemical_labels,
            reservoir_pressure_field[None],
            permeability_field[None],
        ],
        axis=0,
    )
    padded = padded_2(state, (("grp", 1), ("sub", 2)), 1)
    carried_pad = padded[:ncomp]
    press_pad = padded[ncomp]
    perm_pad = padded[ncomp + 1]
    storage_term = (
        pore_capacity * blended_dilution_ratio * chemical_labels - former_chemical_quantity
    )
    resid = all_fluxes(storage_term, carried_pad, press_pad, perm_pad, transmissibility_multipliers)
    block_shape = resid.shape
    p_flat = reservoir_pressure_field.reshape(-1)
    m_flat = relative_flow_ease.reshape(-1)
    z_flat = chemical_labels.reshape(ncomp, -1)
    p_cell = p_flat[perforated_locale]
    m_cell = m_flat[perforated_locale]
    z_cell = z_flat[:, perforated_locale]
    well_group = group_member_place.shape[1]
    segments = conduit_piece_pressures.shape[1]
    owner_row = group_member_place[0]
    well_of = perforated_member[:, 0]
    well_hot = well_of[:, None] == jnp.arange(well_group, dtype=jnp.int32)[None, :]
    slot = jnp.sum(jnp.where(well_hot, owner_row[None, :], 0), axis=1)
    injected = injected_recipe_unnormalized / jnp.sum(injected_recipe_unnormalized)
    table = gathered_copies(conduit_piece_pressures, "sub", 0).reshape(-1)
    random_keys = slot * segments + connection_conduit_piece
    key_hot = random_keys[:, None] == jnp.arange(well_group * segments, dtype=jnp.int32)[None, :]
    p_seg = jnp.sum(jnp.where(key_hot, table[None, :], 0.0), axis=1)
    drop = p_cell - p_seg
    inflow = (connection_inflow_strength * m_cell * drop)[None, :] * jnp.where(
        drop[None, :] > 0, z_cell, injected[:, None]
    )
    totals = jnp.sum(inflow, axis=0)
    partial_rate = jnp.sum(jnp.where(key_hot, totals[:, None], 0.0), axis=0).reshape(
        well_group, segments
    )
    rate = summed_on_arrival(partial_rate, "sub", 0)
    resid_flat = resid.reshape(ncomp, -1).at[:, perforated_locale].add(inflow)
    residual = resid_flat.reshape(block_shape)
    order_hot = (
        conduit_pieces_toe_forward[:, :, None] == jnp.arange(segments)[None, None, :]
    ).astype(jnp.float32)
    ordered = jnp.einsum("wks,ws->wk", order_hot, rate, precision=lax.Precision.HIGHEST)
    upper = (jnp.arange(segments)[:, None] <= jnp.arange(segments)[None, :]).astype(jnp.float32)
    running = jnp.dot(ordered, upper, precision=lax.Precision.HIGHEST)
    press_ord = jnp.einsum(
        "wks,ws->wk", order_hot, conduit_piece_pressures, precision=lax.Precision.HIGHEST
    )
    nexts = jnp.concatenate([press_ord[:, 1:], downstream_exit_pressure[:, None]], axis=1)
    res_ord = press_ord - nexts - friction_factors[:, None] * running * jnp.abs(running)
    well_residual = jnp.einsum("wks,wk->ws", order_hot, res_ord, precision=lax.Precision.HIGHEST)
    return (residual, natural_log_activity.astype(jnp.bfloat16), well_residual)


def solution(mesh):
    in_specs = (
        P(None, "grp", "sub", None),
        P("grp", "sub", None),
        P("grp", "sub", None),
        P("grp", "sub", None),
        P("grp", "sub", None),
        P("grp", "sub", None),
        P(None, "grp", "sub", None),
        P(),
        P(),
        P(),
        P(),
        P(),
        P(),
        P(),
        P(),
        P(("grp", "sub")),
        P(("grp", "sub"), None),
        P(("grp", "sub")),
        P(("grp", "sub")),
        P("grp", None),
        P(("grp", "sub"), None),
        P(("grp", "sub"), None),
        P(("grp", "sub")),
        P(("grp", "sub")),
    )
    out_specs = (P(None, "grp", "sub", None), P(None, "grp", "sub", None), P(("grp", "sub"), None))
    return jax.shard_map(
        per_device, mesh=mesh, in_specs=in_specs, out_specs=out_specs, check_vma=False
    )
```

profile of v0, /device:TPU:1, one launch (start us, length us, event | category | flops | bytes accessed | tf_op | source)
XLA Modules:
  0.0 113.1 jit_solution(2714210947221748205)
XLA Ops:
  0.6 0.0 copy-start.1
  0.6 1.4 %broadcast_in_dim.154 = f32[64,1,32]{2,1,0:T(1,128)} broadcast(f32[32]{0:T(128)} %bitcast.94), dimensions={2} | broadcast | bytes 8320 | tf_op jit(solution)/shard_map/broadcast_in_dim | solution.py:43
  2.0 17.4 %all-to-all-start = ((f32[64,1,32]{2,1,0:T(1,128)}), f32[64,1,32]{2,1,0:T(1,128)}, u32[]{:S(2)}, u32[]{:S(2)}) async-start(f32[64,1,32]{2,1,0:T(1,128)} %broadcast_in_dim.154), calls=%async_computation | async-start | bytes 65536 | tf_op jit(solution)/shard_map/all_to_all | solution.py:42
  19.4 1.3 %fusion.126 = (f32[1]{0:T(128)}, f32[1]{0:T(128)}) fusion(f32[2]{0:T(128)} %param.32), kind=kLoop, calls=%fused_computation.227 | loop fusion | bytes 16 | tf_op jit(solution)/shard_map/slice | solution.py:126
  20.7 0.9 mul.434
  21.7 1.3 %reduce_sum.81 = f32[8,16,128]{2,1,0:T(8,128)S(1)} reduce(f32[16,8,16,128]{3,2,1,0:T(8,128)} %param.24, f32[]{:T(128)} %constant.17.clone.1), dimensions={0}, to_apply=%region_0.0 | reduce | flops 245760 | bytes 1114116 | tf_op jit(solution)/shard_map/reduce_sum | solution.py:76
  23.0 2.1 %fusion.31 = (f32[16,8,16,128]{3,0,2,1:T(8,128)S(1)}, f32[16,8,16,128]{3,0,2,1:T(8,128)S(1)}) fusion(f32[8,16,128]{2,1,0:T(8,128)S(1)} %mul.434, f32[8,16,128]{2,1,0:T(8,128)} %param.25, f32[16]{0:T(128)} %param.33, f32[8,16,128]{2,1,0:T(8,128)} %param.26, f32[16]{0:T(128)} %param.36, f32[16]{0:T(128)} %param.34, f32[8,16,128]{2,1,0:T(8,128)S(1)} %reduce_sum.81, ...), kind=kLoop, calls=%fused_computation.68 | loop fusion | flops 2621440 | bytes 3408064 | tf_op jit(solution)/shard_map/mul | solution.py:94
  25.0 0.3 copy.56
  25.4 0.0 copy-start.15
  25.4 0.0 copy-start.18
  25.4 0.0 copy-start.21
  25.5 0.6 copy.88
  26.1 0.2 copy.75
  26.4 0.0 copy-start.8
  26.4 2.6 %multiply_reduce_fusion = (f32[8,16,128]{2,1,0:T(8,128)S(1)}, f32[8,16,128]{2,1,0:T(8,128)S(1)}, f32[16,8,16,128]{3,0,2,1:T(8,128)S(1)}) fusion(f32[16,8,16,128]{3,0,2,1:T(8,128)S(1)} %get-tuple-element.21, f32[8,16,128]{2,1,0:T(8,128)S(1)} %copy-done.2, f32[8,16,128]{2,1,0:T(8,128)S(1)} %copy-done, f32[16]{0:T(128)S(1)} %copy-done.15, ...), kind=kOutput, calls=%fused_computation.64 | convolution fusion | flops 54231296 | bytes 3474688 | tf_op jit(solution)/shard_map/dot_general | solution.py:92
  29.0 0.4 fusion.124
  29.4 1.4 %subtract_log_fusion = (f32[8,16,128]{2,1,0:T(8,128)S(1)}, f32[8,16,128]{2,1,0:T(8,128)S(1)}, f32[8,16,128]{2,1,0:T(8,128)S(1)}, f32[8,16,128]{2,1,0:T(8,128)S(1)}) fusion(f32[8,16,128]{2,1,0:T(8,128)S(1)} %get-tuple-element.47, f32[8,16,128]{2,1,0:T(8,128)S(1)} %get-tuple-element.16, f32[8,16,128]{2,1,0:T(8,128)S(1)} %copy-done, ...), kind=kLoop, calls=%fused_computation.155 | loop fusion | flops 196608 | bytes 606216 | tf_op jit(solution)/shard_map/log | solution.py:118
  30.8 0.0 copy-start.3
  30.8 0.8 fusion.30
  31.6 0.0 copy-start.22
  31.6 0.0 copy-start.13
  31.6 0.0 copy-start.14
  31.7 0.7 pad_maximum_fusion.18
  32.4 1.3 %collective-permute-start.3 = (f32[18,8,1,128]{3,0,2,1:T(8,128)}, f32[18,8,1,128]{3,0,2,1:T(8,128)}, u32[]{:S(2)}, u32[]{:S(2)}) collective-permute-start(f32[18,8,1,128]{3,0,2,1:T(8,128)} %get-tuple-element.24), channel_id=1, source_target_pairs={{1,0},{2,1},{3,2},{4,3},{5,4},{6,5},{7,6},{8,7},{9,8},{10,9},{11,1... | collective-permute-start | bytes 221192 | tf_op jit(solution)/shard_map/ppermute | solution.py:23
  33.7 4.0 %collective-permute-start = (f32[18,8,1,128]{3,0,2,1:T(8,128)}, f32[18,8,1,128]{3,0,2,1:T(8,128)S(1)}, u32[]{:S(2)}, u32[]{:S(2)}) collective-permute-start(f32[18,8,1,128]{3,0,2,1:T(8,128)} %get-tuple-element.25), channel_id=1, source_target_pairs={{0,1},{1,2},{2,3},{3,4},{4,5},{5,6},{6,7},{7,8},{8,9},{9,10},{10,1... | collective-permute-start | bytes 221192 | tf_op jit(solution)/shard_map/ppermute | solution.py:22
  37.7 0.8 pad_maximum_fusion.17
  38.5 4.5 %collective-permute-start.1 = (f32[18,1,16,128]{3,0,2,1:T(8,128)}, f32[18,1,16,128]{3,0,2,1:T(8,128)S(1)}, u32[]{:S(2)}, u32[]{:S(2)}) collective-permute-start(f32[18,1,16,128]{3,0,2,1:T(8,128)} %get-tuple-element.26), channel_id=1, source_target_pairs={{0,64},{64,128},{128,192},{192,256},{256,320},{320,384},{384,448},... | collective-permute-start | bytes 442376 | tf_op jit(solution)/shard_map/ppermute | solution.py:22
  43.0 1.9 %collective-permute-start.2 = (f32[18,1,16,128]{3,0,2,1:T(8,128)}, f32[18,1,16,128]{3,0,2,1:T(8,128)S(1)}, u32[]{:S(2)}, u32[]{:S(2)}) collective-permute-start(f32[18,1,16,128]{3,0,2,1:T(8,128)} %get-tuple-element.27), channel_id=1, source_target_pairs={{64,0},{128,64},{192,128},{256,192},{320,256},{384,320},{448,384},... | collective-permute-start | bytes 442376 | tf_op jit(solution)/shard_map/ppermute | solution.py:23
  44.9 0.6 reduce_sum.86
  45.5 0.6 broadcast_divide_fusion
  46.2 0.2 fusion.110
  46.4 0.7 slice_bitcast_fusion
  47.1 0.1 select_reduce_fusion.2
  47.2 4.6 %copy.69 = f32[16,8,16,128]{0,3,2,1:T(8,128)} copy(f32[16,8,16,128]{3,0,2,1:T(8,128)S(1)} %get-tuple-element.21) | data formatting | bytes 2097152 | tf_op jit(solution)/shard_map/reshape | solution.py:266
  51.8 1.7 %gather_fusion.1 = f32[256]{0:T(256)S(1)} fusion(f32[16384]{0:T(1024)S(1)} %bitcast.76, s32[1024]{0:T(1024)S(1)} %pad_clamp_fusion), kind=kCustom, calls=%fused_computation.1 | custom fusion | bytes 3072 | tf_op jit(solution)/shard_map/gather | solution.py:267
  53.5 1.7 %gather_fusion = f32[256]{0:T(256)S(1)} fusion(f32[16384]{0:T(1024)S(1)} %bitcast.81, s32[1024]{0:T(1024)S(1)} %pad_clamp_fusion), kind=kCustom, calls=%fused_computation | custom fusion | bytes 3072 | tf_op jit(solution)/shard_map/gather | solution.py:268
  55.3 4.1 %gather_fusion.2 = f32[256,16]{1,0:T(8,128)S(1)} fusion(f32[16,16384]{0,1:T(8,128)} %bitcast.82, s32[1024]{0:T(1024)S(1)} %pad_clamp_fusion), kind=kCustom, calls=%fused_computation.2 | custom fusion | bytes 33792 | tf_op jit(solution)/shard_map/gather | solution.py:269
  59.4 0.5 broadcast.173
  59.9 1.5 %reduce.5 = f32[64,32]{1,0:T(8,128)S(1)} reduce(f32[64,1,32]{2,1,0:T(1,128)} %all-to-all-done, f32[]{:T(128)} %broadcast.173), dimensions={1}, to_apply=%all_to_all.6.reduce_sub_computation.3 | reduce | bytes 16388 | tf_op jit(solution)/shard_map/all_to_all | solution.py:42
  61.4 0.1 broadcast_in_dim.155
  61.5 0.4 select_reduce_fusion.1
  61.9 0.2 fusion.33
  62.1 0.3 select_reduce_fusion
  62.5 0.7 reshape_reshape.3
  63.1 12.5 %all-to-all-start.1 = ((f32[64,1,32]{2,1,0:T(1,128)}), f32[64,1,32]{2,1,0:T(1,128)S(1)}, u32[]{:S(2)}, u32[]{:S(2)}) async-start(f32[64,1,32]{2,1,0:T(1,128)} %bitcast.25), calls=%async_computation.1 | async-start | bytes 65536 | tf_op jit(solution)/shard_map/all_to_all | solution.py:58
  75.7 0.6 fusion.125
  79.5 0.9 copy.66
  80.5 5.9 %all-to-all-done.1 = f32[64,1,32]{2,1,0:T(1,128)S(1)} async-done(((f32[64,1,32]{2,1,0:T(1,128)}), f32[64,1,32]{2,1,0:T(1,128)S(1)}, u32[]{:S(2)}, u32[]{:S(2)}) %all-to-all-start.1) | async-done | bytes 8224 | tf_op jit(solution)/shard_map/all_to_all | solution.py:58
  86.4 0.1 reduce_sum.89
  86.4 0.2 convolution_bitcast_fusion.1
  86.6 0.8 fusion.119
  87.4 0.7 fusion.108
  88.2 0.9 pad.22
  89.1 0.0 copy-start.4
  89.1 0.0 copy-start.5
  89.1 0.2 pad_maximum_fusion.27
  89.5 0.1 subtract_multiply_fusion.5
  89.6 0.1 fusion.106
  89.7 0.1 subtract_multiply_fusion.1
  89.8 0.6 copy-done.4
  90.4 3.6 %fusion.14 = f32[16,8,16,128]{3,0,2,1:T(8,128)S(1)} fusion(f32[16,8,16,128]{3,0,2,1:T(8,128)S(1)} %get-tuple-element.60, f32[18,10,1,128]{3,0,2,1:T(8,128)S(1)} %pad.21, f32[18,1,16,128]{3,0,2,1:T(8,128)} %copy-done.5, f32[18,1,16,128]{3,0,2,1:T(8,128)S(1)} %collective-permute-done.1, f32[1,8,16,128]{3,0,2,1:T(1,128)S(1)} %bitcast.91, ...), kind=kLoop, calls=%fused_computation.29 | loop fusion | flops 9437184 | bytes 5361664 | tf_op jit(solution)/shard_map/add | solution.py:194
  94.0 4.6 %copy.68 = f32[16,8,16,128]{0,3,2,1:T(8,128)} copy(f32[16,8,16,128]{3,0,2,1:T(8,128)S(1)} %fusion.14) | data formatting | bytes 2097152 | tf_op jit(solution)/shard_map/reshape | solution.py:290
  98.6 8.5 %scatter_custom_fusion = f32[16,16384]{0,1:T(8,128)} fusion(f32[16,16384]{0,1:T(8,128)} %bitcast.79, s32[256]{0:T(256)S(1)} %compare_select_fusion, f32[256,16]{1,0:T(8,128)S(1)} %copy-done.7, f32[256]{0:T(256)S(1)} %multiply_multiply_fusion.2, f32[16]{0:T(128)S(1)} %broadcast_divide_fusion, pred[256]{0:T(512)(128)(4,1)S(1)} %broadcast_compare_fusion.1), kind=kCustom, calls=%fused_computation.78 | custom fusion | flops 12288 | bytes 1181696 | tf_op jit(solution)/shard_map/scatter-add | solution.py:290
  107.1 6.1 %copy.65 = f32[16,8,16,128]{3,2,1,0:T(8,128)} copy(f32[16,8,16,128]{0,3,2,1:T(8,128)} %bitcast.80) | data formatting | bytes 2097152
  (51 shorter events, 0.2 us)
Async XLA Ops:
  0.6 22.3 %copy-start.1 = (f32[16,8,16,128]{3,2,1,0:T(8,128)S(1)}, f32[16,8,16,128]{3,2,1,0:T(8,128)}, u32[]{:S(2)}) copy-start(f32[16,8,16,128]{3,2,1,0:T(8,128)} %param.24) | copy-start | bytes 3145732
  2.0 57.4 %all-to-all-start = ((f32[64,1,32]{2,1,0:T(1,128)}), f32[64,1,32]{2,1,0:T(1,128)}, u32[]{:S(2)}, u32[]{:S(2)}) async-start(f32[64,1,32]{2,1,0:T(1,128)} %broadcast_in_dim.154), calls=%async_computation | async-start | bytes 65536 | tf_op jit(solution)/shard_map/all_to_all | solution.py:42
  25.4 0.9 copy-start
  25.4 0.9 copy-start.2
  25.4 0.9 copy-start.15
  25.4 0.9 copy-start.18
  25.4 0.9 copy-start.19
  25.4 0.9 copy-start.20
  25.4 0.9 copy-start.21
  26.4 2.7 %copy-start.8 = (s32[8,16,128]{2,1,0:T(8,128)S(1)}, s32[8,16,128]{2,1,0:T(8,128)}, u32[]{:S(2)}) copy-start(s32[8,16,128]{2,1,0:T(8,128)} %param.27) | copy-start | bytes 196612
  26.4 3.0 %copy-start.9 = (f32[8,16,128]{2,1,0:T(8,128)S(1)}, f32[8,16,128]{2,1,0:T(8,128)}, u32[]{:S(2)}) copy-start(f32[8,16,128]{2,1,0:T(8,128)} %param.29) | copy-start | bytes 196612
  30.8 0.9 copy-start.3
  31.6 13.3 %copy-start.22 = (f32[16]{0:T(128)S(1)}, f32[16]{0:T(128)}, u32[]{:S(2)}) copy-start(f32[16]{0:T(128)} %param.38) | copy-start | bytes 196
  31.6 14.6 %copy-start.16 = (f32[1,32]{1,0:T(1,128)S(1)}, f32[1,32]{1,0:T(1,128)}, u32[]{:S(2)}) copy-start(f32[1,32]{1,0:T(1,128)} %param.45) | copy-start | bytes 388
  31.6 14.6 %copy-start.23 = (s32[1,32]{1,0:T(1,128)S(1)}, s32[1,32]{1,0:T(1,128)}, u32[]{:S(2)}) copy-start(s32[1,32]{1,0:T(1,128)} %param.44) | copy-start | bytes 388
  31.6 15.5 %copy-start.13 = (s32[256]{0:T(256)S(1)}, s32[256]{0:T(256)}, u32[]{:S(2)}) copy-start(s32[256]{0:T(256)} %param.39) | copy-start | bytes 3076
  31.6 15.5 %copy-start.14 = (s32[256,1]{0,1:T(1,128)S(1)}, s32[256,1]{0,1:T(1,128)}, u32[]{:S(2)}) copy-start(s32[256,1]{0,1:T(1,128)} %param.40) | copy-start | bytes 3076
  31.6 15.4 %copy-start.17 = (s32[1,64]{1,0:T(1,128)S(1)}, s32[1,64]{1,0:T(1,128)}, u32[]{:S(2)}) copy-start(s32[1,64]{1,0:T(1,128)} %param.43) | copy-start | bytes 772
  31.7 15.5 %copy-start.11 = (s32[256]{0:T(256)S(1)}, s32[256]{0:T(256)}, u32[]{:S(2)}) copy-start(s32[256]{0:T(256)} %param.41) | copy-start | bytes 3076
  32.4 55.8 %collective-permute-start.3 = (f32[18,8,1,128]{3,0,2,1:T(8,128)}, f32[18,8,1,128]{3,0,2,1:T(8,128)}, u32[]{:S(2)}, u32[]{:S(2)}) collective-permute-start(f32[18,8,1,128]{3,0,2,1:T(8,128)} %get-tuple-element.24), channel_id=1, source_target_pairs={{1,0},{2,1},{3,2},{4,3},{5,4},{6,5},{7,6},{8,7},{9,8},{10,9},{11,1... | collective-permute-start | bytes 221192 | tf_op jit(solution)/shard_map/ppermute | solution.py:23
  33.7 55.4 %collective-permute-start = (f32[18,8,1,128]{3,0,2,1:T(8,128)}, f32[18,8,1,128]{3,0,2,1:T(8,128)S(1)}, u32[]{:S(2)}, u32[]{:S(2)}) collective-permute-start(f32[18,8,1,128]{3,0,2,1:T(8,128)} %get-tuple-element.25), channel_id=1, source_target_pairs={{0,1},{1,2},{2,3},{3,4},{4,5},{5,6},{6,7},{7,8},{8,9},{9,10},{10,1... | collective-permute-start | bytes 221192 | tf_op jit(solution)/shard_map/ppermute | solution.py:22
  38.5 50.6 %collective-permute-start.1 = (f32[18,1,16,128]{3,0,2,1:T(8,128)}, f32[18,1,16,128]{3,0,2,1:T(8,128)S(1)}, u32[]{:S(2)}, u32[]{:S(2)}) collective-permute-start(f32[18,1,16,128]{3,0,2,1:T(8,128)} %get-tuple-element.26), channel_id=1, source_target_pairs={{0,64},{64,128},{128,192},{192,256},{256,320},{320,384},{384,448},... | collective-permute-start | bytes 442376 | tf_op jit(solution)/shard_map/ppermute | solution.py:22
  43.0 46.1 %collective-permute-start.2 = (f32[18,1,16,128]{3,0,2,1:T(8,128)}, f32[18,1,16,128]{3,0,2,1:T(8,128)S(1)}, u32[]{:S(2)}, u32[]{:S(2)}) collective-permute-start(f32[18,1,16,128]{3,0,2,1:T(8,128)} %get-tuple-element.27), channel_id=1, source_target_pairs={{64,0},{128,64},{192,128},{256,192},{320,256},{384,320},{448,384},... | collective-permute-start | bytes 442376 | tf_op jit(solution)/shard_map/ppermute | solution.py:23
  51.8 10.1 %copy-start.12 = (f32[256]{0:T(256)S(1)}, f32[256]{0:T(256)}, u32[]{:S(2)}) copy-start(f32[256]{0:T(256)} %param.42) | copy-start | bytes 3076
  51.8 23.9 %copy-start.10 = (f32[3]{0:T(128)S(1)}, f32[3]{0:T(128)}, u32[]{:S(2)}) copy-start(f32[3]{0:T(128)} %param.31) | copy-start | bytes 40
  59.4 30.0 %copy-start.6 = (f32[256,16]{1,0:T(8,128)}, f32[256,16]{1,0:T(8,128)S(1)}, u32[]{:S(2)}) copy-start(f32[256,16]{1,0:T(8,128)S(1)} %gather_fusion.2) | copy-start | bytes 49156
  63.1 23.2 %all-to-all-start.1 = ((f32[64,1,32]{2,1,0:T(1,128)}), f32[64,1,32]{2,1,0:T(1,128)S(1)}, u32[]{:S(2)}, u32[]{:S(2)}) async-start(f32[64,1,32]{2,1,0:T(1,128)} %bitcast.25), calls=%async_computation.1 | async-start | bytes 65536 | tf_op jit(solution)/shard_map/all_to_all | solution.py:58
  89.1 1.3 %copy-start.4 = (f32[16,8,16,128]{3,2,1,0:T(8,128)S(1)}, f32[16,8,16,128]{3,2,1,0:T(8,128)}, u32[]{:S(2)}) copy-start(f32[16,8,16,128]{3,2,1,0:T(8,128)} %param.30) | copy-start | bytes 3145732
  89.1 0.7 copy-start.5
  94.0 4.6 %copy-start.7 = (f32[256,16]{1,0:T(8,128)S(1)}, f32[256,16]{1,0:T(8,128)}, u32[]{:S(2)}) copy-start(f32[256,16]{1,0:T(8,128)} %copy-done.6) | copy-start | bytes 49156
where the time goes:
time: 115 us; the launch traced here: 113 us
  starting transfers between devices  41.6 us (36%)
  local copies, waits for them, and re-layouts  31.8 us (28%)
  other arithmetic  24.8 us (22%)
  waiting for transfers between devices  5.9 us (5%)
  matrix products  4.56 us (4%)
  between operations  4.43 us (4%)
    all_to_all x1, starting transfers between devices, from_everyone(): lax.all_to_all(jnp.broadcast_to(array[None], (size, *array.shape)), axis,...  17.4 us
    all_to_all x1, starting transfers between devices, summed_on_arrival(): lax.all_to_all(pieces, axis, split_axis=0, concat_axis=0, tiled=True)  12.5 us
    unnamed x54, local copies, waits for them, and re-layouts  8.52 us
    ppermute x2, starting transfers between devices, padded_2(): lax.ppermute(last, axis, up)  8.5 us
    scatter-add x1, other arithmetic, per_device(): resid_flat = resid.reshape(ncomp, -1).at[:, perforated_locale].add(inflow)  8.49 us
    all_to_all x1, waiting for transfers between devices, summed_on_arrival(): lax.all_to_all(pieces, axis, split_axis=0, concat_axis=0, tiled=True)  5.89 us
    reshape x1, local copies, waits for them, and re-layouts, per_device(): resid_flat = resid.reshape(ncomp, -1).at[:, perforated_locale].add(inflow)  4.6 us
    reshape x1, local copies, waits for them, and re-layouts, per_device(): z_flat = chemical_labels.reshape(ncomp, -1)  4.6 us
  transfers between devices with their start and end apart: 6, of which 1 were waited for; matrix products, arithmetic and copies ran while one was open for 32% of the time, Pallas kernels for 0%

commit v1 on v0

v1 whole, which is shorter than its diff:
```python
import functools
import math

import jax
import jax.numpy as jnp
from jax import lax
from jax.experimental import pallas as pl
from jax.experimental.pallas import tpu as pltpu
from jax.sharding import PartitionSpec as P

NEWT = 8
ROOT_TWO = math.sqrt(2.0)
MESH = pl.DeviceIdType.MESH
NC = 16
CX = 8
CY = 16
LANES = 128
LINE = 8
SMALL = 15
SCALARS = 8
F32 = jnp.float32
BF16 = jnp.bfloat16
HIGHEST = lax.Precision.HIGHEST


def iota(shape, axis):
    return lax.broadcasted_iota(jnp.int32, shape, axis)


def hot(index_row, rows):
    mask = iota((rows, index_row.shape[1]), 0) == index_row
    return jnp.where(mask, 1.0, 0.0).astype(F32)


def pieces_of(x, count):
    out = []
    for _ in range(count):
        top = x.astype(BF16)
        out.append(top)
        x = x - top.astype(F32)
    return out


def mm(a, b):
    return lax.dot_general(a, b, (((1,), (0,)), ((), ())), preferred_element_type=F32)


def mm_nt(a, b):
    return lax.dot_general(a, b, (((1,), (1,)), ((), ())), preferred_element_type=F32)


def mm_full(a, b):
    return lax.dot_general(
        a, b, (((1,), (0,)), ((), ())), precision=HIGHEST, preferred_element_type=F32
    )


def mm_full_nt(a, b):
    return lax.dot_general(
        a, b, (((1,), (1,)), ((), ())), precision=HIGHEST, preferred_element_type=F32
    )


def pick_rows(field, lane_hot, row_mask, count):
    parts = pieces_of(field, count)
    found = mm(jnp.concatenate(parts, axis=0), lane_hot)
    rows = field.shape[0]
    total = found[:rows]
    for i in range(1, count):
        total = total + found[i * rows : (i + 1) * rows]
    return jnp.sum(jnp.where(row_mask, total, 0.0), axis=0, keepdims=True)


def body(
    n_grp,
    n_sub,
    n_hbm,
    p_hbm,
    t_hbm,
    flag_hbm,
    k_hbm,
    pore_hbm,
    old_hbm,
    *refs,
):
    small_hbm, refs = refs[:SMALL], refs[SMALL:]
    exit_p, friction, *refs = refs
    resid_ref, lnphi_ref, well_ref = refs[:3]
    small_refs, refs = refs[3 : 3 + SMALL], refs[3 + SMALL :]
    (
        trans,
        visc,
        crit,
        attract,
        covol,
        kappa,
        kij,
        recipe,
        loc_ref,
        mem_ref,
        seg_ref,
        wi_ref,
        gmp_ref,
        order_ref,
        cpp_ref,
    ) = small_refs
    (
        n_v,
        t_v,
        flag_v,
        pore_v,
        old_v,
        st,
        um_v,
        w_v,
        mob_v,
        e1_v,
        e2_v,
        e3_v,
        pv_v,
        wp_v,
        wn_v,
        c0_t,
        c1_t,
        cb_t,
        inj_t,
        row_v,
        ag1_src,
        ag1,
        ag2_src,
        ag2,
        rs1_src,
        rs1,
        rs2_src,
        rs2,
        ys_lo,
        ys_hi,
        yr_lo,
        yr_hi,
        in_sem,
        send_sem,
        recv_sem,
        halo_send,
        halo_recv,
        small_sem,
    ) = refs
    g = lax.axis_index("grp")
    s = lax.axis_index("sub")
    z, y = s // LINE, s % LINE

    def z_peer(d):
        return {"sub": ((z + d) % LINE) * LINE + y}

    def y_peer(d):
        return {"sub": z * LINE + (y + d) % LINE}

    g_up, g_down = {"grp": (g + 1) % n_grp}, {"grp": (g + n_grp - 1) % n_grp}
    s_up, s_down = {"sub": (s + 1) % n_sub}, {"sub": (s + n_sub - 1) % n_sub}

    inner = pl.ds(1, CX)
    rows = pl.ds(8, CY)
    half = CX // 2
    loads = [
        pltpu.make_async_copy(t_hbm, t_v, in_sem.at[0]),
        pltpu.make_async_copy(p_hbm, st.at[NC, inner, rows], in_sem.at[1]),
        pltpu.make_async_copy(n_hbm.at[:, pl.ds(0, half)], n_v.at[:, pl.ds(0, half)], in_sem.at[2]),
        pltpu.make_async_copy(
            n_hbm.at[:, pl.ds(half, half)], n_v.at[:, pl.ds(half, half)], in_sem.at[3]
        ),
        pltpu.make_async_copy(flag_hbm, flag_v, in_sem.at[4]),
        pltpu.make_async_copy(k_hbm, st.at[NC + 1, inner, rows], in_sem.at[5]),
        pltpu.make_async_copy(pore_hbm, pore_v, in_sem.at[6]),
        pltpu.make_async_copy(old_hbm, old_v, in_sem.at[7]),
    ]
    small_loads = [
        pltpu.make_async_copy(src, dst, small_sem.at[i])
        for i, (src, dst) in enumerate(zip(small_hbm, small_refs))
    ]
    for load in small_loads + loads:
        load.start()

    barrier = pltpu.get_barrier_semaphore()
    peers = [z_peer(d) for d in range(1, LINE)] + [y_peer(d) for d in range(1, LINE)]
    peers += [g_up, g_down, s_up, s_down]
    for peer in peers:
        pl.semaphore_signal(barrier, inc=1, device_id=peer, device_id_type=MESH)

    for load in small_loads:
        load.wait()

    tile = (8, LANES)
    total = jnp.zeros(tile, F32)
    for i in range(NC):
        total = total + recipe[i]
    for i in range(NC):
        amount = jnp.sqrt(jnp.full(tile, attract[i], F32))
        slope = jnp.full(tile, kappa[i], F32)
        c0_t[i] = amount * (1.0 + slope)
        c1_t[i] = amount * slope / jnp.sqrt(jnp.full(tile, crit[i], F32))
        cb_t[i] = jnp.full(tile, covol[i], F32)
        inj_t[i] = jnp.full(tile, recipe[i], F32) / total

    row_v[...] = jnp.zeros(tile, F32)
    row_v[0:1, 0:32] = cpp_ref[...]
    own_row = row_v[0:1, :]
    ag1_src[...] = jnp.where(iota(tile, 0) == y, own_row, 0.0)

    loc = [loc_ref[h : h + 1, :] for h in range(2)]
    row_of = jnp.concatenate([v // LANES for v in loc], axis=1)
    lane_of = jnp.concatenate([v % LANES for v in loc], axis=1)
    member = jnp.concatenate([mem_ref[h : h + 1, :] for h in range(2)], axis=1)
    segment = jnp.concatenate([seg_ref[h : h + 1, :] for h in range(2)], axis=1)
    strength = jnp.concatenate([wi_ref[h : h + 1, :] for h in range(2)], axis=1)
    wells = n_sub
    place = jnp.where(iota((wells, wells), 0) == gmp_ref[...], 1.0, 0.0).astype(BF16)
    slot_hot = mm(place, hot(member, wells).astype(BF16))
    lane_hot = hot(lane_of, LANES)
    lane_hot_b = lane_hot.astype(BF16)
    row_mask = iota((LANES, 2 * LANES), 0) == row_of
    row_hot_b = jnp.where(row_mask, 1.0, 0.0).astype(BF16)
    seg_hot = hot(segment, LANES).astype(BF16)
    seg_hot_2 = hot(segment + 32, LANES).astype(BF16)

    order = jnp.where(iota((32, 32), 0) == order_ref[...], 1.0, 0.0).astype(F32)
    sub32, lane32 = iota((32, 32), 0), iota((32, 32), 1)
    upper = jnp.where(sub32 <= lane32, 1.0, 0.0).astype(F32)
    after = jnp.where(sub32 == lane32 + 1, 1.0, 0.0).astype(F32)
    before_hot = mm_full_nt(mm_full(order, upper), order)
    next_hot = mm_full_nt(mm_full(order, after), order)
    last_row = jnp.where(iota((8, 32), 1) == 31, 1.0, 0.0).astype(F32)
    last_hot = mm_full_nt(last_row, order)
    cpp = jnp.broadcast_to(cpp_ref[...], (8, 32))
    base = cpp - (mm_full(cpp, next_hot) + exit_p[0] * last_hot)

    loads[0].wait()
    loads[1].wait()
    loads[4].wait()
    loads[6].wait()

    def phase(b, _):
        xs = pl.ds(b * half, half)
        xp = pl.ds(b * half + 1, half)
        pltpu.make_async_copy(n_hbm.at[:, xs], n_v.at[:, xs], in_sem.at[2 + b]).wait()
        t = t_v[xs]
        p = st[NC, xp, rows, :]
        root_t = jnp.sqrt(t)
        whole = jnp.zeros_like(t)
        bsum = jnp.zeros_like(t)

        def wide(table, i):
            v = table[i]
            return jnp.broadcast_to(
                jnp.concatenate([v, v], axis=0)[None], (half, CY, LANES)
            )

        for i in range(NC):
            n = n_v[i, xs]
            u = jnp.abs(wide(c0_t, i) - wide(c1_t, i) * root_t)
            um_v[i, xs] = u
            w_v[i] = n * u
            whole = whole + n
            bsum = bsum + wide(cb_t, i) * n
        asum = jnp.zeros_like(t)
        for i in range(NC):
            m = None
            for j in range(NC):
                term = w_v[j] * (1.0 - kij[i, j])
                m = term if m is None else m + term
            um = um_v[i, xs] * m
            um_v[i, xs] = um
            asum = asum + n_v[i, xs] * um
        inv = 1.0 / whole
        inv_t = 1.0 / t
        pt = p * inv_t
        gain = pt * inv_t * inv
        big_a = gain * inv * asum
        big_b = pt * inv * bsum
        liquid = flag_v[xs] == 1
        zed = jnp.where(liquid, big_b + 0.01, 1.0 + big_b)
        low = big_b + 0.01
        c2 = big_b - 1.0
        c2x2 = 2.0 * c2
        c1 = big_a - 3.0 * big_b * big_b - 2.0 * big_b
        c0 = big_b * big_b + big_b * big_b * big_b - big_a * big_b
        for _step in range(NEWT):
            value = ((zed + c2) * zed + c1) * zed + c0
            slope = (3.0 * zed + c2x2) * zed + c1
            zed = jnp.maximum(zed - value / jnp.maximum(slope, 0.1), low)
        ratio = jnp.log((zed + (1.0 + ROOT_TWO) * big_b) / (zed + (1.0 - ROOT_TWO) * big_b))
        inv_b = 1.0 / big_b
        e3 = ratio * inv_b * (1.0 / ROOT_TWO)
        e1_v[xs] = pt * inv_b * ((zed - 1.0) + 0.5 * big_a * e3)
        e2_v[xs] = jnp.log(zed - big_b)
        e3_v[xs] = e3 * gain
        thick = jnp.where(liquid, visc[1], visc[0])
        mob = pt / (zed * thick)
        mob_v[xs] = mob
        pv_v[xs] = pore_v[xs] * thick
        share = mob * inv
        for i in range(NC):
            st[i, xp, rows, :] = n_v[i, xs] * share
        return 0

    lax.fori_loop(0, 2, phase, 0)

    pl.semaphore_wait(barrier, len(peers))

    def tile_copy(src, dst, kind, slot, peer):
        return pltpu.make_async_remote_copy(
            src_ref=src,
            dst_ref=dst,
            send_sem=send_sem.at[kind, slot],
            recv_sem=recv_sem.at[kind, slot],
            device_id=peer,
            device_id_type=MESH,
        )

    ag1_copies = [tile_copy(ag1_src, ag1.at[d], 0, d, y_peer(d)) for d in range(1, LINE)]
    for copy in ag1_copies:
        copy.start()

    p_cell = pick_rows(
        st[NC, inner, rows, :].reshape(LANES, LANES), lane_hot_b, row_mask, 3
    )
    mob_cell = pick_rows(mob_v[...].reshape(LANES, LANES), lane_hot_b, row_mask, 2)
    v0 = strength * mob_cell
    v1 = v0 * (p_cell - 1.0)
    left = jnp.concatenate([slot_hot * v0, slot_hot * v1], axis=1)
    right = jnp.concatenate([seg_hot, seg_hot_2], axis=1)
    sums = None
    for part in pieces_of(left, 3):
        found = mm_nt(part, right)
        sums = found if sums is None else sums + found
    rs1_src[...] = sums.reshape(LINE, LINE, LANES)
    rs1_copies = [
        tile_copy(rs1_src.at[(z + d) % LINE], rs1.at[d], 2, d, z_peer(d)) for d in range(1, LINE)
    ]
    for copy in rs1_copies:
        copy.start()

    loads[5].wait()

    def gather_rows(c, _):
        ys_lo[c] = st[c, inner, 8, :]
        ys_hi[c] = st[c, inner, 8 + CY - 1, :]
        return 0

    lax.fori_loop(0, NC + 2, gather_rows, 0)

    def halo_copy(src, dst, slot, peer):
        return pltpu.make_async_remote_copy(
            src_ref=src,
            dst_ref=dst,
            send_sem=halo_send.at[slot],
            recv_sem=halo_recv.at[slot],
            device_id=peer,
            device_id_type=MESH,
        )

    halo_copies = [
        halo_copy(st.at[:, CX, rows], st.at[:, 0, rows], 0, g_up),
        halo_copy(st.at[:, 1, rows], st.at[:, CX + 1, rows], 1, g_down),
        halo_copy(ys_hi, yr_lo, 2, s_up),
        halo_copy(ys_lo, yr_hi, 3, s_down),
    ]
    for copy in halo_copies:
        copy.start()

    for copy in ag1_copies:
        copy.wait_recv()
    line = ag1_src[...]
    for d in range(1, LINE):
        line = line + ag1[d]
    ag2_src[...] = line
    ag2_copies = [tile_copy(ag2_src, ag2.at[z], 1, d, z_peer(d)) for d in range(1, LINE)]
    for copy in ag2_copies:
        copy.start()
    ag2[z] = line

    def fugacity(x, _):
        e1, e2, e3 = e1_v[x], e2_v[x], e3_v[x]
        for i in range(NC):
            v = cb_t[i]
            cb = jnp.concatenate([v, v], axis=0)
            lnphi_ref[i, x] = (cb * e1 - e2 - um_v[i, x] * e3).astype(BF16)
        return 0

    lax.fori_loop(0, CX, fugacity, 0)

    for copy in rs1_copies:
        copy.wait_recv()
    part = rs1_src[z]
    for d in range(1, LINE):
        part = part + rs1[d]
    rs2_src[...] = part
    rs2_copies = [tile_copy(rs2_src, rs2.at[d], 3, d, y_peer(d)) for d in range(1, LINE)]
    for copy in rs2_copies:
        copy.start()

    for d in range(1, LINE):
        tile_copy(ag2_src, ag2.at[(z + LINE - d) % LINE], 1, d, z_peer(d)).wait_recv()
    table = ag2[...].reshape(LINE * LINE, LANES)
    p_seg = pick_rows(table, seg_hot, slot_hot > 0.5, 3)
    push = strength * (p_cell - p_seg)
    push_up, push_down = jnp.maximum(push, 0.0), jnp.minimum(push, 0.0)
    spread = jnp.concatenate([lane_hot * push_up, lane_hot * push_down], axis=0)
    dense = None
    for part in pieces_of(spread, 3):
        found = mm_nt(row_hot_b, part)
        dense = found if dense is None else dense + found
    wp_v[...] = dense[:, :LANES].reshape(CX, CY, LANES)
    wn_v[...] = dense[:, LANES:].reshape(CX, CY, LANES)

    for copy in halo_copies:
        copy.wait_recv()

    def put_rows(c, _):
        st[c, inner, 7, :] = yr_lo[c]
        st[c, inner, 8 + CY, :] = yr_hi[c]
        return 0

    lax.fori_loop(0, NC + 2, put_rows, 0)
    loads[7].wait()

    plane = (CY, LANES)
    y_id, lane_id = iota(plane, 0), iota(plane, 1)
    has_low = jnp.logical_or(y_id > 0, s > 0)
    has_high = jnp.logical_or(y_id < CY - 1, s < n_sub - 1)

    def flux(x, _):
        xc = x + 1
        p, k = st[NC, xc, rows, :], st[NC + 1, xc, rows, :]

        def side(p_b, k_b, factor):
            trans_ab = factor * 2.0 * k * k_b / (k + k_b)
            flow = trans_ab * (p - p_b)
            return jnp.maximum(flow, 0.0), jnp.minimum(flow, 0.0)

        f_low = jnp.where(jnp.logical_or(x > 0, g > 0), trans[0], 0.0)
        f_high = jnp.where(jnp.logical_or(x < CX - 1, g < n_grp - 1), trans[0], 0.0)
        up_rows, down_rows = pl.ds(9, CY), pl.ds(7, CY)
        faces = [
            side(st[NC, xc - 1, rows, :], st[NC + 1, xc - 1, rows, :], f_low),
            side(st[NC, xc + 1, rows, :], st[NC + 1, xc + 1, rows, :], f_high),
            side(
                st[NC, xc, down_rows, :],
                st[NC + 1, xc, down_rows, :],
                jnp.where(has_low, trans[1], 0.0),
            ),
            side(
                st[NC, xc, up_rows, :],
                st[NC + 1, xc, up_rows, :],
                jnp.where(has_high, trans[1], 0.0),
            ),
            side(
                pltpu.roll(p, 1, 1),
                pltpu.roll(k, 1, 1),
                jnp.where(lane_id > 0, trans[2], 0.0),
            ),
            side(
                pltpu.roll(p, LANES - 1, 1),
                pltpu.roll(k, LANES - 1, 1),
                jnp.where(lane_id < LANES - 1, trans[2], 0.0),
            ),
        ]
        diag = pv_v[x] + wp_v[x]
        for out, _in in faces:
            diag = diag + out
        gain = mob_v[x] * wn_v[x]
        coming = [f[1] for f in faces]
        for i in range(NC):
            v = inj_t[i]
            inj = jnp.concatenate([v, v], axis=0)
            c = st[i, xc, rows, :]
            r = c * diag + gain * inj - old_v[i, x]
            r = r + coming[0] * st[i, xc - 1, rows, :]
            r = r + coming[1] * st[i, xc + 1, rows, :]
            r = r + coming[2] * st[i, xc, down_rows, :]
            r = r + coming[3] * st[i, xc, up_rows, :]
            r = r + coming[4] * pltpu.roll(c, 1, 1)
            r = r + coming[5] * pltpu.roll(c, LANES - 1, 1)
            resid_ref[i, x] = r
        return 0

    lax.fori_loop(0, CX, flux, 0)

    for copy in rs2_copies:
        copy.wait_recv()
    full = rs2_src[...]
    for d in range(1, LINE):
        full = full + rs2[d]
    mine = jnp.sum(jnp.where(iota(tile, 0) == y, full, 0.0), axis=0, keepdims=True)
    mine = jnp.broadcast_to(mine, tile)
    row_v[...] = mine
    s0 = row_v[:, 0:32]
    s1 = row_v[:, 32:64]
    rate = s1 - (cpp - 1.0) * s0
    running = mm_full(rate, before_hot)
    well = base - friction[0] * running * jnp.abs(running)
    well_ref[...] = well[0:1]

    for copy in ag1_copies + ag2_copies + rs1_copies + rs2_copies + halo_copies:
        copy.wait_send()


def per_device(n_grp, n_sub, *args):
    (
        amounts,
        pressure,
        heat,
        flag,
        perm,
        pore,
        former,
        trans,
        visc,
        crit,
        attract,
        covol,
        kappa,
        kij,
        recipe,
        locale,
        member,
        piece,
        strength,
        place,
        order,
        seg_pressure,
        exit_pressure,
        friction,
    ) = args
    field = (CX, CY, LANES)
    every = (NC, CX, CY, LANES)
    hbm = pl.BlockSpec(memory_space=pltpu.HBM)
    smem = pl.BlockSpec(memory_space=pltpu.SMEM)
    vmem = pl.BlockSpec(memory_space=pltpu.VMEM)
    tiles = pltpu.VMEM((LINE, 8, LANES), F32)
    one = pltpu.VMEM((8, LANES), F32)
    table = pltpu.VMEM((NC, 8, LANES), F32)
    edge = pltpu.VMEM((NC + 2, CX, LANES), F32)
    scratch = [
        pltpu.VMEM(every, F32),
        pltpu.VMEM(field, F32),
        pltpu.VMEM(field, jnp.int32),
        pltpu.VMEM(field, F32),
        pltpu.VMEM(every, F32),
        pltpu.VMEM((NC + 2, CX + 2, CY + 16, LANES), F32),
        pltpu.VMEM(every, F32),
        pltpu.VMEM((NC, CX // 2, CY, LANES), F32),
        *[pltpu.VMEM(field, F32) for _ in range(7)],
        table,
        table,
        table,
        table,
        one,
        one,
        tiles,
        one,
        tiles,
        tiles,
        tiles,
        one,
        tiles,
        edge,
        edge,
        edge,
        edge,
        pltpu.SemaphoreType.DMA((8,)),
        pltpu.SemaphoreType.DMA((4, LINE)),
        pltpu.SemaphoreType.DMA((4, LINE)),
        pltpu.SemaphoreType.DMA((4,)),
        pltpu.SemaphoreType.DMA((4,)),
        pltpu.SemaphoreType.DMA((SMALL,)),
    ]
    small = (
        trans,
        visc,
        crit,
        attract,
        covol,
        kappa,
        kij,
        recipe,
        locale.reshape(2, LANES),
        member.reshape(2, LANES),
        piece.reshape(2, LANES),
        strength.reshape(2, LANES),
        place,
        order,
        seg_pressure,
    )
    spaces = [pltpu.SMEM] * SCALARS + [pltpu.VMEM] * (SMALL - SCALARS)
    held = [space(v.shape, v.dtype) for space, v in zip(spaces, small)]
    return pl.pallas_call(
        functools.partial(body, n_grp, n_sub),
        out_shape=(
            jax.ShapeDtypeStruct(every, F32),
            jax.ShapeDtypeStruct(every, BF16),
            jax.ShapeDtypeStruct((1, 32), F32),
        ),
        in_specs=[hbm] * (7 + SMALL) + [smem] * 2,
        out_specs=(vmem, vmem, vmem),
        scratch_shapes=held + scratch,
        compiler_params=pltpu.CompilerParams(
            collective_id=0, has_side_effects=True, vmem_limit_bytes=40 * 1024 * 1024
        ),
        name="newton_residual",
    )(
        *[
            pltpu.with_memory_space_constraint(v, pltpu.HBM)
            for v in (amounts, pressure, heat, flag, perm, pore, former, *small)
        ],
        exit_pressure,
        friction,
    )


def solution(mesh):
    areal = P("grp", "sub", None)
    every = P(None, "grp", "sub", None)
    both = P(("grp", "sub"))
    rows = P(("grp", "sub"), None)
    in_specs = (
        every,
        areal,
        areal,
        areal,
        areal,
        areal,
        every,
        *[P()] * 8,
        both,
        rows,
        both,
        both,
        P("grp", None),
        rows,
        rows,
        both,
        both,
    )
    return jax.shard_map(
        functools.partial(per_device, mesh.shape["grp"], mesh.shape["sub"]),
        mesh=mesh,
        in_specs=in_specs,
        out_specs=(every, every, rows),
        check_vma=False,
    )
```

time: 115 us -> 31 us (0.27)
  the two profiles are of different devices: /device:TPU:1 before, /device:TPU:4 now
where the time goes in v1:
time: 31 us; the launch traced here: 30.9 us
  Pallas kernels  26.7 us (86%)
  local copies, waits for them, and re-layouts  2.28 us (7%)
  between operations  1.94 us (6%)
    pallas_call x1, Pallas kernels, per_device(): pl.pallas_call(functools.partial(body, n_grp, n_sub), out_shape=(jax.Shap...  26.7 us
    unnamed x3, local copies, waits for them, and re-layouts  2.28 us

profile of v1, /device:TPU:4, one launch (start us, length us, event | category | flops | bytes accessed | tf_op | source)
XLA Modules:
  0.0 30.9 jit_solution(1480282998994925087)
XLA Ops:
  1.9 26.7 %newton_residual.1 = (f32[16,8,16,128]{3,2,1,0:T(8,128)S(1)}, bf16[16,8,16,128]{3,2,1,0:T(8,128)(2,1)S(1)}, f32[1,32]{1,0:T(1,128)S(1)}) custom-call(f32[16,8,16,128]{3,2,1,0:T(8,128)} %n_hbm.1, f32[8,16,128]{2,1,0:T(8,128)} %p_hbm.1, f32[8,16,128]{2,1,0:T(8,128)} %t_hbm.1, s32[8,16,128]{2,1,0:T(8,128)} %flag_hbm.1, f32[8,16,128]{2,1,0:T(8,128)} %k_hbm.1, ...), custom_call_target="tpu_custom_call" | custom-call | tf_op jit(solution)/shard_map/newton_residual/pallas_call | solution.py:595
  28.6 1.0 %copy.32 = f32[16,8,16,128]{3,2,1,0:T(8,128)} copy(f32[16,8,16,128]{3,2,1,0:T(8,128)S(1)} %get-tuple-element.6) | data formatting | bytes 2097152
  29.6 0.8 %copy.33 = bf16[16,8,16,128]{3,2,1,0:T(8,128)(2,1)} copy(bf16[16,8,16,128]{3,2,1,0:T(8,128)(2,1)S(1)} %get-tuple-element.7) | data formatting | bytes 1048576
  30.4 0.5 %copy.34 = f32[1,32]{1,0:T(1,128)} copy(f32[1,32]{1,0:T(1,128)S(1)} %get-tuple-element.8) | data formatting | bytes 256

commit v2 on v1

--- a/solution.py
+++ b/solution.py
@@ -21,6 +21,14 @@
 F32 = jnp.float32
 BF16 = jnp.bfloat16
 HIGHEST = lax.Precision.HIGHEST
+
+
+def away(step):
+    return sum(min(d, LINE - d) for d in step)
+
+
+STEPS = [(dz, dy) for dz in range(LINE) for dy in range(LINE) if dz or dy]
+STEPS.sort(key=away, reverse=True)
 
 
 def iota(shape, axis):
@@ -125,21 +133,15 @@
         cb_t,
         inj_t,
         row_v,
-        ag1_src,
-        ag1,
-        ag2_src,
-        ag2,
-        rs1_src,
-        rs1,
-        rs2_src,
-        rs2,
+        mail_out,
+        mail_in,
         ys_lo,
         ys_hi,
         yr_lo,
         yr_hi,
         in_sem,
-        send_sem,
-        recv_sem,
+        mail_send,
+        mail_recv,
         halo_send,
         halo_recv,
         small_sem,
@@ -148,12 +150,10 @@
     s = lax.axis_index("sub")
     z, y = s // LINE, s % LINE
 
-    def z_peer(d):
-        return {"sub": ((z + d) % LINE) * LINE + y}
-
-    def y_peer(d):
-        return {"sub": z * LINE + (y + d) % LINE}
-
+    def peer_at(dz, dy):
+        return ((z + dz) % LINE) * LINE + (y + dy) % LINE
+
+    mates = [peer_at(dz, dy) for dz, dy in STEPS]
     g_up, g_down = {"grp": (g + 1) % n_grp}, {"grp": (g + n_grp - 1) % n_grp}
     s_up, s_down = {"sub": (s + 1) % n_sub}, {"sub": (s + n_sub - 1) % n_sub}
 
@@ -176,14 +176,17 @@
         pltpu.make_async_copy(src, dst, small_sem.at[i])
         for i, (src, dst) in enumerate(zip(small_hbm, small_refs))
     ]
-    for load in small_loads + loads:
+    for load in small_loads[SCALARS:] + loads[:3]:
         load.start()
+    for load in small_loads[:SCALARS]:
+        load.start()
 
     barrier = pltpu.get_barrier_semaphore()
-    peers = [z_peer(d) for d in range(1, LINE)] + [y_peer(d) for d in range(1, LINE)]
-    peers += [g_up, g_down, s_up, s_down]
+    peers = [{"sub": mate} for mate in mates] + [g_up, g_down]
     for peer in peers:
         pl.semaphore_signal(barrier, inc=1, device_id=peer, device_id_type=MESH)
+    for load in loads[3:]:
+        load.start()
 
     for load in small_loads:
         load.wait()
@@ -201,9 +204,8 @@
         inj_t[i] = jnp.full(tile, recipe[i], F32) / total
 
     row_v[...] = jnp.zeros(tile, F32)
-    row_v[0:1, 0:32] = cpp_ref[...]
+    row_v[0:1, 64:96] = cpp_ref[...]
     own_row = row_v[0:1, :]
-    ag1_src[...] = jnp.where(iota(tile, 0) == y, own_row, 0.0)
 
     loc = [loc_ref[h : h + 1, :] for h in range(2)]
     row_of = jnp.concatenate([v // LANES for v in loc], axis=1)
@@ -220,6 +222,7 @@
     row_hot_b = jnp.where(row_mask, 1.0, 0.0).astype(BF16)
     seg_hot = hot(segment, LANES).astype(BF16)
     seg_hot_2 = hot(segment + 32, LANES).astype(BF16)
+    seg_hot_3 = hot(segment + 64, LANES).astype(BF16)
 
     order = jnp.where(iota((32, 32), 0) == order_ref[...], 1.0, 0.0).astype(F32)
     sub32, lane32 = iota((32, 32), 0), iota((32, 32), 1)
@@ -303,22 +306,6 @@
 
     lax.fori_loop(0, 2, phase, 0)
 
-    pl.semaphore_wait(barrier, len(peers))
-
-    def tile_copy(src, dst, kind, slot, peer):
-        return pltpu.make_async_remote_copy(
-            src_ref=src,
-            dst_ref=dst,
-            send_sem=send_sem.at[kind, slot],
-            recv_sem=recv_sem.at[kind, slot],
-            device_id=peer,
-            device_id_type=MESH,
-        )
-
-    ag1_copies = [tile_copy(ag1_src, ag1.at[d], 0, d, y_peer(d)) for d in range(1, LINE)]
-    for copy in ag1_copies:
-        copy.start()
-
     p_cell = pick_rows(
         st[NC, inner, rows, :].reshape(LANES, LANES), lane_hot_b, row_mask, 3
     )
@@ -331,12 +318,27 @@
     for part in pieces_of(left, 3):
         found = mm_nt(part, right)
         sums = found if sums is None else sums + found
-    rs1_src[...] = sums.reshape(LINE, LINE, LANES)
-    rs1_copies = [
-        tile_copy(rs1_src.at[(z + d) % LINE], rs1.at[d], 2, d, z_peer(d)) for d in range(1, LINE)
-    ]
-    for copy in rs1_copies:
-        copy.start()
+    mail_out[...] = (sums + own_row).reshape(n_sub, 1, LANES)
+    mail_in[s] = mail_out[s]
+
+    pl.semaphore_wait(barrier, len(peers))
+    for mate in mates:
+        pltpu.make_async_remote_copy(
+            src_ref=mail_out.at[mate],
+            dst_ref=mail_in.at[s],
+            send_sem=mail_send,
+            recv_sem=mail_recv,
+            device_id={"sub": mate},
+            device_id_type=MESH,
+        ).start()
+    mail = pltpu.make_async_remote_copy(
+        src_ref=mail_out.at[pl.ds(0, n_sub - 1)],
+        dst_ref=mail_in.at[pl.ds(0, n_sub - 1)],
+        send_sem=mail_send,
+        recv_sem=mail_recv,
+        device_id=g_up,
+        device_id_type=MESH,
+    )
 
     loads[5].wait()
 
@@ -366,17 +368,6 @@
     for copy in halo_copies:
         copy.start()
 
-    for copy in ag1_copies:
-        copy.wait_recv()
-    line = ag1_src[...]
-    for d in range(1, LINE):
-        line = line + ag1[d]
-    ag2_src[...] = line
-    ag2_copies = [tile_copy(ag2_src, ag2.at[z], 1, d, z_peer(d)) for d in range(1, LINE)]
-    for copy in ag2_copies:
-        copy.start()
-    ag2[z] = line
-
     def fugacity(x, _):
         e1, e2, e3 = e1_v[x], e2_v[x], e3_v[x]
         for i in range(NC):
@@ -386,30 +377,6 @@
         return 0
 
     lax.fori_loop(0, CX, fugacity, 0)
-
-    for copy in rs1_copies:
-        copy.wait_recv()
-    part = rs1_src[z]
-    for d in range(1, LINE):
-        part = part + rs1[d]
-    rs2_src[...] = part
-    rs2_copies = [tile_copy(rs2_src, rs2.at[d], 3, d, y_peer(d)) for d in range(1, LINE)]
-    for copy in rs2_copies:
-        copy.start()
-
-    for d in range(1, LINE):
-        tile_copy(ag2_src, ag2.at[(z + LINE - d) % LINE], 1, d, z_peer(d)).wait_recv()
-    table = ag2[...].reshape(LINE * LINE, LANES)
-    p_seg = pick_rows(table, seg_hot, slot_hot > 0.5, 3)
-    push = strength * (p_cell - p_seg)
-    push_up, push_down = jnp.maximum(push, 0.0), jnp.minimum(push, 0.0)
-    spread = jnp.concatenate([lane_hot * push_up, lane_hot * push_down], axis=0)
-    dense = None
-    for part in pieces_of(spread, 3):
-        found = mm_nt(row_hot_b, part)
-        dense = found if dense is None else dense + found
-    wp_v[...] = dense[:, :LANES].reshape(CX, CY, LANES)
-    wn_v[...] = dense[:, LANES:].reshape(CX, CY, LANES)
 
     for copy in halo_copies:
         copy.wait_recv()
@@ -463,16 +430,13 @@
                 jnp.where(lane_id < LANES - 1, trans[2], 0.0),
             ),
         ]
-        diag = pv_v[x] + wp_v[x]
+        diag = pv_v[x]
         for out, _in in faces:
             diag = diag + out
-        gain = mob_v[x] * wn_v[x]
         coming = [f[1] for f in faces]
         for i in range(NC):
-            v = inj_t[i]
-            inj = jnp.concatenate([v, v], axis=0)
             c = st[i, xc, rows, :]
-            r = c * diag + gain * inj - old_v[i, x]
+            r = c * diag - old_v[i, x]
             r = r + coming[0] * st[i, xc - 1, rows, :]
             r = r + coming[1] * st[i, xc + 1, rows, :]
             r = r + coming[2] * st[i, xc, down_rows, :]
@@ -484,23 +448,48 @@
 
     lax.fori_loop(0, CX, flux, 0)
 
-    for copy in rs2_copies:
-        copy.wait_recv()
-    full = rs2_src[...]
-    for d in range(1, LINE):
-        full = full + rs2[d]
-    mine = jnp.sum(jnp.where(iota(tile, 0) == y, full, 0.0), axis=0, keepdims=True)
-    mine = jnp.broadcast_to(mine, tile)
-    row_v[...] = mine
-    s0 = row_v[:, 0:32]
-    s1 = row_v[:, 32:64]
-    rate = s1 - (cpp - 1.0) * s0
+    for copy in halo_copies:
+        copy.wait_send()
+    mail.wait_send()
+
+    mail.wait_recv()
+    table = mail_in[...].reshape(n_sub, LANES)
+    p_seg = pick_rows(table, seg_hot_3, slot_hot > 0.5, 3)
+    push = strength * (p_cell - p_seg)
+    push_up, push_down = jnp.maximum(push, 0.0), jnp.minimum(push, 0.0)
+    spread = jnp.concatenate([lane_hot * push_up, lane_hot * push_down], axis=0)
+    dense = None
+    for part in pieces_of(spread, 2):
+        found = mm_nt(row_hot_b, part)
+        dense = found if dense is None else dense + found
+    wp_v[...] = dense[:, :LANES].reshape(CX, CY, LANES)
+    wn_v[...] = dense[:, LANES:].reshape(CX, CY, LANES)
+
+    mine = jnp.sum(table, axis=0, keepdims=True)
+    row_v[...] = jnp.broadcast_to(mine, tile)
+    rate = row_v[:, 32:64] - (cpp - 1.0) * row_v[:, 0:32]
     running = mm_full(rate, before_hot)
     well = base - friction[0] * running * jnp.abs(running)
     well_ref[...] = well[0:1]
 
-    for copy in ag1_copies + ag2_copies + rs1_copies + rs2_copies + halo_copies:
-        copy.wait_send()
+    def perforated(x, _):
+        wp, gain = wp_v[x], mob_v[x] * wn_v[x]
+        for i in range(NC):
+            v = inj_t[i]
+            inj = jnp.concatenate([v, v], axis=0)
+            resid_ref[i, x] = resid_ref[i, x] + (st[i, x + 1, rows, :] * wp + gain * inj)
+        return 0
+
+    lax.fori_loop(0, CX, perforated, 0)
+
+
+def put(resid, lnphi, well, resid_out, lnphi_out, well_out, sem):
+    pairs = ((resid, resid_out), (lnphi, lnphi_out), (well, well_out))
+    copies = [pltpu.make_async_copy(a, b, sem.at[i]) for i, (a, b) in enumerate(pairs)]
+    for copy in copies:
+        copy.start()
+    for copy in copies:
+        copy.wait()
 
 
 def per_device(n_grp, n_sub, *args):
@@ -535,7 +524,7 @@
     hbm = pl.BlockSpec(memory_space=pltpu.HBM)
     smem = pl.BlockSpec(memory_space=pltpu.SMEM)
     vmem = pl.BlockSpec(memory_space=pltpu.VMEM)
-    tiles = pltpu.VMEM((LINE, 8, LANES), F32)
+    mail = pltpu.VMEM((n_sub, 1, LANES), F32)
     one = pltpu.VMEM((8, LANES), F32)
     table = pltpu.VMEM((NC, 8, LANES), F32)
     edge = pltpu.VMEM((NC + 2, CX, LANES), F32)
@@ -554,21 +543,15 @@
         table,
         table,
         one,
-        one,
-        tiles,
-        one,
-        tiles,
-        tiles,
-        tiles,
-        one,
-        tiles,
+        mail,
+        mail,
         edge,
         edge,
         edge,
         edge,
         pltpu.SemaphoreType.DMA((8,)),
-        pltpu.SemaphoreType.DMA((4, LINE)),
-        pltpu.SemaphoreType.DMA((4, LINE)),
+        pltpu.SemaphoreType.DMA,
+        pltpu.SemaphoreType.DMA,
         pltpu.SemaphoreType.DMA((4,)),
         pltpu.SemaphoreType.DMA((4,)),
         pltpu.SemaphoreType.DMA((SMALL,)),
@@ -592,13 +575,14 @@
     )
     spaces = [pltpu.SMEM] * SCALARS + [pltpu.VMEM] * (SMALL - SCALARS)
     held = [space(v.shape, v.dtype) for space, v in zip(spaces, small)]
-    return pl.pallas_call(
+    outs = (
+        jax.ShapeDtypeStruct(every, F32),
+        jax.ShapeDtypeStruct(every, BF16),
+        jax.ShapeDtypeStruct((1, 32), F32),
+    )
+    found = pl.pallas_call(
         functools.partial(body, n_grp, n_sub),
-        out_shape=(
-            jax.ShapeDtypeStruct(every, F32),
-            jax.ShapeDtypeStruct(every, BF16),
-            jax.ShapeDtypeStruct((1, 32), F32),
-        ),
+        out_shape=outs,
         in_specs=[hbm] * (7 + SMALL) + [smem] * 2,
         out_specs=(vmem, vmem, vmem),
         scratch_shapes=held + scratch,
@@ -614,6 +598,15 @@
         exit_pressure,
         friction,
     )
+    return pl.pallas_call(
+        put,
+        out_shape=outs,
+        in_specs=[vmem] * 3,
+        out_specs=(hbm,) * 3,
+        scratch_shapes=[pltpu.SemaphoreType.DMA((3,))],
+        compiler_params=pltpu.CompilerParams(vmem_limit_bytes=4 * 1024 * 1024),
+        name="put_outputs",
+    )(*found)
 
 
 def solution(mesh):

time: 31 us -> 27.3 us (0.88)
  the two profiles are of different devices: /device:TPU:4 before, /device:TPU:1 now
where the time goes in v2:
time: 27.3 us; the launch traced here: 27.2 us
  Pallas kernels  25.2 us (92%)
  between operations  1.94 us (7%)
    pallas_call x1, Pallas kernels, per_device(): pl.pallas_call(functools.partial(body, n_grp, n_sub), out_shape=outs, in_...  24 us
    pallas_call x1, Pallas kernels, per_device(): pl.pallas_call(put, out_shape=outs, in_specs=[vmem] * 3, out_specs=(hbm,)...  1.17 us

profile of v2, /device:TPU:1, one launch (start us, length us, event | category | flops | bytes accessed | tf_op | source)
XLA Modules:
  0.0 27.2 jit_solution(8423123599662755294)
XLA Ops:
  1.9 24.0 %newton_residual.1 = (f32[16,8,16,128]{3,2,1,0:T(8,128)S(1)}, bf16[16,8,16,128]{3,2,1,0:T(8,128)(2,1)S(1)}, f32[1,32]{1,0:T(1,128)S(1)}) custom-call(f32[16,8,16,128]{3,2,1,0:T(8,128)} %n_hbm.1, f32[8,16,128]{2,1,0:T(8,128)} %p_hbm.1, f32[8,16,128]{2,1,0:T(8,128)} %t_hbm.1, s32[8,16,128]{2,1,0:T(8,128)} %flag_hbm.1, f32[8,16,128]{2,1,0:T(8,128)} %k_hbm.1, ...), custom_call_target="tpu_custom_call" | custom-call | tf_op jit(solution)/shard_map/newton_residual/pallas_call | solution.py:583
  26.0 1.2 %put_outputs.1 = (f32[16,8,16,128]{3,2,1,0:T(8,128)}, bf16[16,8,16,128]{3,2,1,0:T(8,128)(2,1)}, f32[1,32]{1,0:T(1,128)}) custom-call(f32[16,8,16,128]{3,2,1,0:T(8,128)S(1)} %get-tuple-element.6.resid, bf16[16,8,16,128]{3,2,1,0:T(8,128)(2,1)S(1)} %get-tuple-element.7.lnphi, f32[1,32]{1,0:T(1,128)S(1)} %get-tuple-element.8.well), custom_call_target="tpu_custom_call" | custom-call | tf_op jit(solution)/shard_map/put_outputs/pallas_call | solution.py:601

commit v3 on v2

--- a/solution.py
+++ b/solution.py
@@ -21,14 +21,6 @@
 F32 = jnp.float32
 BF16 = jnp.bfloat16
 HIGHEST = lax.Precision.HIGHEST
-
-
-def away(step):
-    return sum(min(d, LINE - d) for d in step)
-
-
-STEPS = [(dz, dy) for dz in range(LINE) for dy in range(LINE) if dz or dy]
-STEPS.sort(key=away, reverse=True)
 
 
 def iota(shape, axis):
@@ -119,13 +111,19 @@
         pore_v,
         old_v,
         st,
-        um_v,
+        up_v,
         w_v,
         mob_v,
         e1_v,
         e2_v,
         e3_v,
-        pv_v,
+        root_v,
+        inv_v,
+        pt_v,
+        gain_v,
+        a_v,
+        b_v,
+        z_v,
         wp_v,
         wn_v,
         c0_t,
@@ -142,20 +140,18 @@
         in_sem,
         mail_send,
         mail_recv,
+        ready,
         halo_send,
         halo_recv,
         small_sem,
     ) = refs
     g = lax.axis_index("grp")
     s = lax.axis_index("sub")
-    z, y = s // LINE, s % LINE
-
-    def peer_at(dz, dy):
-        return ((z + dz) % LINE) * LINE + (y + dy) % LINE
-
-    mates = [peer_at(dz, dy) for dz, dy in STEPS]
     g_up, g_down = {"grp": (g + 1) % n_grp}, {"grp": (g + n_grp - 1) % n_grp}
     s_up, s_down = {"sub": (s + 1) % n_sub}, {"sub": (s + n_sub - 1) % n_sub}
+    line = s // LINE
+    has_g_up, has_g_down = g < n_grp - 1, g > 0
+    has_s_up, has_s_down = s < n_sub - 1, s > 0
 
     inner = pl.ds(1, CX)
     rows = pl.ds(8, CY)
@@ -176,35 +172,46 @@
         pltpu.make_async_copy(src, dst, small_sem.at[i])
         for i, (src, dst) in enumerate(zip(small_hbm, small_refs))
     ]
-    for load in small_loads[SCALARS:] + loads[:3]:
+    for load in small_loads + loads[:4]:
         load.start()
-    for load in small_loads[:SCALARS]:
-        load.start()
 
     barrier = pltpu.get_barrier_semaphore()
-    peers = [{"sub": mate} for mate in mates] + [g_up, g_down]
-    for peer in peers:
-        pl.semaphore_signal(barrier, inc=1, device_id=peer, device_id_type=MESH)
-    for load in loads[3:]:
+
+    def greet(there, peer):
+        @pl.when(there)
+        def _():
+            pl.semaphore_signal(barrier, inc=1, device_id=peer, device_id_type=MESH)
+
+    def greet_higher(j, _):
+        pl.semaphore_signal(barrier, inc=1, device_id={"sub": j}, device_id_type=MESH)
+        return 0
+
+    greet(has_g_up, g_up)
+    greet(has_g_down, g_down)
+    greet(has_s_down, s_down)
+    lax.fori_loop(s + 1, n_sub, greet_higher, 0)
+    expected = (
+        s
+        + has_s_up.astype(jnp.int32)
+        + has_g_up.astype(jnp.int32)
+        + has_g_down.astype(jnp.int32)
+    )
+    for load in loads[4:]:
         load.start()
 
     for load in small_loads:
         load.wait()
 
     tile = (8, LANES)
-    total = jnp.zeros(tile, F32)
-    for i in range(NC):
-        total = total + recipe[i]
     for i in range(NC):
         amount = jnp.sqrt(jnp.full(tile, attract[i], F32))
         slope = jnp.full(tile, kappa[i], F32)
         c0_t[i] = amount * (1.0 + slope)
         c1_t[i] = amount * slope / jnp.sqrt(jnp.full(tile, crit[i], F32))
         cb_t[i] = jnp.full(tile, covol[i], F32)
-        inj_t[i] = jnp.full(tile, recipe[i], F32) / total
 
     row_v[...] = jnp.zeros(tile, F32)
-    row_v[0:1, 64:96] = cpp_ref[...]
+    row_v[0:1, 64:96] = cpp_ref[...] - 1.0
     own_row = row_v[0:1, :]
 
     loc = [loc_ref[h : h + 1, :] for h in range(2)]
@@ -224,6 +231,168 @@
     seg_hot_2 = hot(segment + 32, LANES).astype(BF16)
     seg_hot_3 = hot(segment + 64, LANES).astype(BF16)
 
+    def wide(table, i):
+        v = table[i]
+        return jnp.broadcast_to(jnp.concatenate([v, v], axis=0)[None], (half, CY, LANES))
+
+    loads[0].wait()
+    loads[1].wait()
+
+    def phase(b, _):
+        xs = pl.ds(b * half, half)
+        xp = pl.ds(b * half + 1, half)
+        pltpu.make_async_copy(n_hbm.at[:, xs], n_v.at[:, xs], in_sem.at[2 + b]).wait()
+        t = t_v[xs]
+        root_t = jnp.sqrt(t)
+        root_v[xs] = root_t
+        whole = jnp.zeros_like(t)
+        bsum = jnp.zeros_like(t)
+        for i in range(NC):
+            n = n_v[i, xs]
+            w_v[i, xs] = n * jnp.abs(wide(c0_t, i) - wide(c1_t, i) * root_t)
+            whole = whole + n
+            bsum = bsum + wide(cb_t, i) * n
+        last = w_v[NC - 1, xs]
+        asum = last * last
+        for i in range(NC - 1):
+            m = None
+            for j in range(i + 1, NC):
+                term = w_v[j, xs] * (1.0 - kij[i, j])
+                m = term if m is None else m + term
+            up_v[i, xs] = m
+            w = w_v[i, xs]
+            asum = asum + w * (w + 2.0 * m)
+        inv = 1.0 / whole
+        inv_t = 1.0 / t
+        pt = st[NC, xp, rows, :] * inv_t
+        gain = pt * inv_t * inv
+        inv_v[xs] = inv
+        pt_v[xs] = pt
+        gain_v[xs] = gain
+        a_v[xs] = gain * inv * asum
+        b_v[xs] = pt * inv * bsum
+        return 0
+
+    lax.fori_loop(0, 2, phase, 0)
+
+    loads[4].wait()
+    big_a, big_b = a_v[...], b_v[...]
+    liquid = flag_v[...] == 1
+    zed = jnp.where(liquid, big_b + 0.01, 1.0 + big_b)
+    c1 = big_a - 3.0 * big_b * big_b - 2.0 * big_b
+    c0 = big_b * big_b + big_b * big_b * big_b - big_a * big_b
+    for _step in range(NEWT):
+        c2 = big_b - 1.0
+        value = ((zed + c2) * zed + c1) * zed + c0
+        slope = (3.0 * zed + 2.0 * c2) * zed + c1
+        zed = jnp.maximum(zed - value / jnp.maximum(slope, 0.1), big_b + 0.01)
+    z_v[...] = zed
+    mob_v[...] = pt_v[...] / (zed * jnp.where(liquid, visc[1], visc[0]))
+
+    p_cell = pick_rows(
+        st[NC, inner, rows, :].reshape(LANES, LANES) - 1.0, lane_hot_b, row_mask, 2
+    )
+    mob_cell = pick_rows(mob_v[...].reshape(LANES, LANES), lane_hot_b, row_mask, 2)
+    v0 = strength * mob_cell
+    v1 = v0 * p_cell
+    left = jnp.concatenate([slot_hot * v0, slot_hot * v1], axis=1)
+    right = jnp.concatenate([seg_hot, seg_hot_2], axis=1)
+    sums = None
+    for part in pieces_of(left, 2):
+        found = mm_nt(part, right)
+        sums = found if sums is None else sums + found
+    mail_out[...] = (sums + own_row).reshape(n_sub, 1, LANES)
+    mail_in[s] = mail_out[s]
+
+    def post(j, _):
+        pltpu.make_async_remote_copy(
+            src_ref=mail_out.at[j],
+            dst_ref=mail_in.at[s],
+            send_sem=mail_send,
+            recv_sem=mail_recv,
+            device_id={"sub": j},
+            device_id_type=MESH,
+        ).start()
+        return 0
+
+    def tell(j, _):
+        pl.semaphore_signal(
+            ready.at[line], inc=1, device_id={"sub": j}, device_id_type=MESH
+        )
+        return 0
+
+    pl.semaphore_wait(barrier, expected)
+    lax.fori_loop(0, s, post, 0)
+    lax.fori_loop(0, s, tell, 0)
+    mail = pltpu.make_async_remote_copy(
+        src_ref=mail_out.at[pl.ds(0, n_sub - 1)],
+        dst_ref=mail_in.at[pl.ds(0, n_sub - 1)],
+        send_sem=mail_send,
+        recv_sem=mail_recv,
+        device_id=g_up,
+        device_id_type=MESH,
+    )
+
+    def carry(x, _):
+        share = mob_v[x] * inv_v[x]
+        for i in range(NC):
+            st[i, x + 1, rows, :] = n_v[i, x] * share
+        return 0
+
+    lax.fori_loop(0, CX, carry, 0)
+    loads[5].wait()
+
+    def gather_rows(c, _):
+        ys_lo[c] = st[c, inner, 8, :]
+        ys_hi[c] = st[c, inner, 8 + CY - 1, :]
+        return 0
+
+    lax.fori_loop(0, NC + 2, gather_rows, 0)
+
+    def halo_copy(src, dst, slot, peer):
+        return pltpu.make_async_remote_copy(
+            src_ref=src,
+            dst_ref=dst,
+            send_sem=halo_send.at[slot],
+            recv_sem=halo_recv.at[slot],
+            device_id=peer,
+            device_id_type=MESH,
+        )
+
+    halo_copies = [
+        halo_copy(st.at[:, CX, rows], st.at[:, 0, rows], 0, g_up),
+        halo_copy(st.at[:, 1, rows], st.at[:, CX + 1, rows], 1, g_down),
+        halo_copy(ys_hi, yr_lo, 2, s_up),
+        halo_copy(ys_lo, yr_hi, 3, s_down),
+    ]
+    sends = (has_g_up, has_g_down, has_s_up, has_s_down)
+    receives = (has_g_down, has_g_up, has_s_down, has_s_up)
+
+    for there, copy in zip(sends, halo_copies):
+        pl.when(there)(copy.start)
+
+    @pl.when(jnp.logical_not(has_g_down))
+    def _():
+        st[:, 0, rows, :] = jnp.zeros((NC + 2, CY, LANES), F32)
+
+    @pl.when(jnp.logical_not(has_g_up))
+    def _():
+        st[:, CX + 1, rows, :] = jnp.zeros((NC + 2, CY, LANES), F32)
+
+    @pl.when(jnp.logical_not(has_s_down))
+    def _():
+        yr_lo[...] = jnp.zeros((NC + 2, CX, LANES), F32)
+
+    @pl.when(jnp.logical_not(has_s_up))
+    def _():
+        yr_hi[...] = jnp.zeros((NC + 2, CX, LANES), F32)
+
+    total = jnp.zeros(tile, F32)
+    for i in range(NC):
+        total = total + recipe[i]
+    for i in range(NC):
+        inj_t[i] = jnp.full(tile, recipe[i], F32) / total
+
     order = jnp.where(iota((32, 32), 0) == order_ref[...], 1.0, 0.0).astype(F32)
     sub32, lane32 = iota((32, 32), 0), iota((32, 32), 1)
     upper = jnp.where(sub32 <= lane32, 1.0, 0.0).astype(F32)
@@ -235,151 +404,34 @@
     cpp = jnp.broadcast_to(cpp_ref[...], (8, 32))
     base = cpp - (mm_full(cpp, next_hot) + exit_p[0] * last_hot)
 
-    loads[0].wait()
-    loads[1].wait()
-    loads[4].wait()
+
     loads[6].wait()
 
-    def phase(b, _):
+    def fugacity(b, _):
         xs = pl.ds(b * half, half)
-        xp = pl.ds(b * half + 1, half)
-        pltpu.make_async_copy(n_hbm.at[:, xs], n_v.at[:, xs], in_sem.at[2 + b]).wait()
-        t = t_v[xs]
-        p = st[NC, xp, rows, :]
-        root_t = jnp.sqrt(t)
-        whole = jnp.zeros_like(t)
-        bsum = jnp.zeros_like(t)
-
-        def wide(table, i):
-            v = table[i]
-            return jnp.broadcast_to(
-                jnp.concatenate([v, v], axis=0)[None], (half, CY, LANES)
-            )
-
-        for i in range(NC):
-            n = n_v[i, xs]
-            u = jnp.abs(wide(c0_t, i) - wide(c1_t, i) * root_t)
-            um_v[i, xs] = u
-            w_v[i] = n * u
-            whole = whole + n
-            bsum = bsum + wide(cb_t, i) * n
-        asum = jnp.zeros_like(t)
-        for i in range(NC):
-            m = None
-            for j in range(NC):
-                term = w_v[j] * (1.0 - kij[i, j])
-                m = term if m is None else m + term
-            um = um_v[i, xs] * m
-            um_v[i, xs] = um
-            asum = asum + n_v[i, xs] * um
-        inv = 1.0 / whole
-        inv_t = 1.0 / t
-        pt = p * inv_t
-        gain = pt * inv_t * inv
-        big_a = gain * inv * asum
-        big_b = pt * inv * bsum
-        liquid = flag_v[xs] == 1
-        zed = jnp.where(liquid, big_b + 0.01, 1.0 + big_b)
-        low = big_b + 0.01
-        c2 = big_b - 1.0
-        c2x2 = 2.0 * c2
-        c1 = big_a - 3.0 * big_b * big_b - 2.0 * big_b
-        c0 = big_b * big_b + big_b * big_b * big_b - big_a * big_b
-        for _step in range(NEWT):
-            value = ((zed + c2) * zed + c1) * zed + c0
-            slope = (3.0 * zed + c2x2) * zed + c1
-            zed = jnp.maximum(zed - value / jnp.maximum(slope, 0.1), low)
+        zed, big_b, pt = z_v[xs], b_v[xs], pt_v[xs]
         ratio = jnp.log((zed + (1.0 + ROOT_TWO) * big_b) / (zed + (1.0 - ROOT_TWO) * big_b))
         inv_b = 1.0 / big_b
         e3 = ratio * inv_b * (1.0 / ROOT_TWO)
-        e1_v[xs] = pt * inv_b * ((zed - 1.0) + 0.5 * big_a * e3)
+        e1_v[xs] = pt * inv_b * ((zed - 1.0) + 0.5 * a_v[xs] * e3)
         e2_v[xs] = jnp.log(zed - big_b)
-        e3_v[xs] = e3 * gain
-        thick = jnp.where(liquid, visc[1], visc[0])
-        mob = pt / (zed * thick)
-        mob_v[xs] = mob
-        pv_v[xs] = pore_v[xs] * thick
-        share = mob * inv
+        e3_v[xs] = e3 * gain_v[xs]
+        pore_v[xs] = pore_v[xs] * jnp.where(flag_v[xs] == 1, visc[1], visc[0])
         for i in range(NC):
-            st[i, xp, rows, :] = n_v[i, xs] * share
-        return 0
-
-    lax.fori_loop(0, 2, phase, 0)
-
-    p_cell = pick_rows(
-        st[NC, inner, rows, :].reshape(LANES, LANES), lane_hot_b, row_mask, 3
-    )
-    mob_cell = pick_rows(mob_v[...].reshape(LANES, LANES), lane_hot_b, row_mask, 2)
-    v0 = strength * mob_cell
-    v1 = v0 * (p_cell - 1.0)
-    left = jnp.concatenate([slot_hot * v0, slot_hot * v1], axis=1)
-    right = jnp.concatenate([seg_hot, seg_hot_2], axis=1)
-    sums = None
-    for part in pieces_of(left, 3):
-        found = mm_nt(part, right)
-        sums = found if sums is None else sums + found
-    mail_out[...] = (sums + own_row).reshape(n_sub, 1, LANES)
-    mail_in[s] = mail_out[s]
-
-    pl.semaphore_wait(barrier, len(peers))
-    for mate in mates:
-        pltpu.make_async_remote_copy(
-            src_ref=mail_out.at[mate],
-            dst_ref=mail_in.at[s],
-            send_sem=mail_send,
-            recv_sem=mail_recv,
-            device_id={"sub": mate},
-            device_id_type=MESH,
-        ).start()
-    mail = pltpu.make_async_remote_copy(
-        src_ref=mail_out.at[pl.ds(0, n_sub - 1)],
-        dst_ref=mail_in.at[pl.ds(0, n_sub - 1)],
-        send_sem=mail_send,
-        recv_sem=mail_recv,
-        device_id=g_up,
-        device_id_type=MESH,
-    )
-
-    loads[5].wait()
-
-    def gather_rows(c, _):
-        ys_lo[c] = st[c, inner, 8, :]
-        ys_hi[c] = st[c, inner, 8 + CY - 1, :]
-        return 0
-
-    lax.fori_loop(0, NC + 2, gather_rows, 0)
-
-    def halo_copy(src, dst, slot, peer):
-        return pltpu.make_async_remote_copy(
-            src_ref=src,
-            dst_ref=dst,
-            send_sem=halo_send.at[slot],
-            recv_sem=halo_recv.at[slot],
-            device_id=peer,
-            device_id_type=MESH,
-        )
-
-    halo_copies = [
-        halo_copy(st.at[:, CX, rows], st.at[:, 0, rows], 0, g_up),
-        halo_copy(st.at[:, 1, rows], st.at[:, CX + 1, rows], 1, g_down),
-        halo_copy(ys_hi, yr_lo, 2, s_up),
-        halo_copy(ys_lo, yr_hi, 3, s_down),
-    ]
-    for copy in halo_copies:
-        copy.start()
-
-    def fugacity(x, _):
-        e1, e2, e3 = e1_v[x], e2_v[x], e3_v[x]
-        for i in range(NC):
-            v = cb_t[i]
-            cb = jnp.concatenate([v, v], axis=0)
-            lnphi_ref[i, x] = (cb * e1 - e2 - um_v[i, x] * e3).astype(BF16)
-        return 0
-
-    lax.fori_loop(0, CX, fugacity, 0)
-
-    for copy in halo_copies:
-        copy.wait_recv()
+            m = w_v[i, xs]
+            if i < NC - 1:
+                m = m + up_v[i, xs]
+            for j in range(i):
+                m = m + w_v[j, xs] * (1.0 - kij[i, j])
+            u = jnp.abs(wide(c0_t, i) - wide(c1_t, i) * root_v[xs])
+            part = wide(cb_t, i) * e1_v[xs] - e2_v[xs]
+            lnphi_ref[i, xs] = (part - u * m * e3_v[xs]).astype(BF16)
+        return 0
+
+    lax.fori_loop(0, 2, fugacity, 0)
+
+    for there, copy in zip(receives, halo_copies):
+        pl.when(there)(copy.wait_recv)
 
     def put_rows(c, _):
         st[c, inner, 7, :] = yr_lo[c]
@@ -390,9 +442,7 @@
     loads[7].wait()
 
     plane = (CY, LANES)
-    y_id, lane_id = iota(plane, 0), iota(plane, 1)
-    has_low = jnp.logical_or(y_id > 0, s > 0)
-    has_high = jnp.logical_or(y_id < CY - 1, s < n_sub - 1)
+    lane_id = iota(plane, 1)
 
     def flux(x, _):
         xc = x + 1
@@ -403,21 +453,19 @@
             flow = trans_ab * (p - p_b)
             return jnp.maximum(flow, 0.0), jnp.minimum(flow, 0.0)
 
-        f_low = jnp.where(jnp.logical_or(x > 0, g > 0), trans[0], 0.0)
-        f_high = jnp.where(jnp.logical_or(x < CX - 1, g < n_grp - 1), trans[0], 0.0)
         up_rows, down_rows = pl.ds(9, CY), pl.ds(7, CY)
         faces = [
-            side(st[NC, xc - 1, rows, :], st[NC + 1, xc - 1, rows, :], f_low),
-            side(st[NC, xc + 1, rows, :], st[NC + 1, xc + 1, rows, :], f_high),
+            side(st[NC, xc - 1, rows, :], st[NC + 1, xc - 1, rows, :], trans[0]),
+            side(st[NC, xc + 1, rows, :], st[NC + 1, xc + 1, rows, :], trans[0]),
             side(
                 st[NC, xc, down_rows, :],
                 st[NC + 1, xc, down_rows, :],
-                jnp.where(has_low, trans[1], 0.0),
+                trans[1],
             ),
             side(
                 st[NC, xc, up_rows, :],
                 st[NC + 1, xc, up_rows, :],
-                jnp.where(has_high, trans[1], 0.0),
+                trans[1],
             ),
             side(
                 pltpu.roll(p, 1, 1),
@@ -430,7 +478,7 @@
                 jnp.where(lane_id < LANES - 1, trans[2], 0.0),
             ),
         ]
-        diag = pv_v[x]
+        diag = pore_v[x]
         for out, _in in faces:
             diag = diag + out
         coming = [f[1] for f in faces]
@@ -448,13 +496,20 @@
 
     lax.fori_loop(0, CX, flux, 0)
 
-    for copy in halo_copies:
-        copy.wait_send()
+    def post_line(k, _):
+        first = jnp.maximum(s + 1, k * LINE)
+        pl.semaphore_wait(ready.at[k], (k + 1) * LINE - first)
+        lax.fori_loop(first, (k + 1) * LINE, post, 0)
+        return 0
+
+    lax.fori_loop((s + 1) // LINE, n_sub // LINE, post_line, 0)
+    for there, copy in zip(sends, halo_copies):
+        pl.when(there)(copy.wait_send)
     mail.wait_send()
 
     mail.wait_recv()
     table = mail_in[...].reshape(n_sub, LANES)
-    p_seg = pick_rows(table, seg_hot_3, slot_hot > 0.5, 3)
+    p_seg = pick_rows(table, seg_hot_3, slot_hot > 0.5, 2)
     push = strength * (p_cell - p_seg)
     push_up, push_down = jnp.maximum(push, 0.0), jnp.minimum(push, 0.0)
     spread = jnp.concatenate([lane_hot * push_up, lane_hot * push_down], axis=0)
@@ -536,8 +591,8 @@
         pltpu.VMEM(every, F32),
         pltpu.VMEM((NC + 2, CX + 2, CY + 16, LANES), F32),
         pltpu.VMEM(every, F32),
-        pltpu.VMEM((NC, CX // 2, CY, LANES), F32),
-        *[pltpu.VMEM(field, F32) for _ in range(7)],
+        pltpu.VMEM(every, F32),
+        *[pltpu.VMEM(field, F32) for _ in range(13)],
         table,
         table,
         table,
@@ -552,6 +607,7 @@
         pltpu.SemaphoreType.DMA((8,)),
         pltpu.SemaphoreType.DMA,
         pltpu.SemaphoreType.DMA,
+        pltpu.SemaphoreType.REGULAR((n_sub // LINE,)),
         pltpu.SemaphoreType.DMA((4,)),
         pltpu.SemaphoreType.DMA((4,)),
         pltpu.SemaphoreType.DMA((SMALL,)),

time: 27.3 us -> 24.3 us (0.89)
  Pallas kernels: 25.2 us -> 22.2 us
    pallas_call x1, Pallas kernels: 24 us -> 21 us  [per_device(): pl.pallas_call(functools.partial(body, n_grp, n_sub), out_shape=outs, in_...]
where the time goes in v3:
time: 24.3 us; the launch traced here: 24.1 us
  Pallas kernels  22.2 us (91%)
  between operations  1.94 us (8%)
    pallas_call x1, Pallas kernels, per_device(): pl.pallas_call(functools.partial(body, n_grp, n_sub), out_shape=outs, in_...  21 us
    pallas_call x1, Pallas kernels, per_device(): pl.pallas_call(put, out_shape=outs, in_specs=[vmem] * 3, out_specs=(hbm,)...  1.17 us

profile of v3, /device:TPU:1, one launch (start us, length us, event | category | flops | bytes accessed | tf_op | source)
XLA Modules:
  0.0 24.1 jit_solution(17666844346363430625)
XLA Ops:
  1.9 21.0 %newton_residual.1 = (f32[16,8,16,128]{3,2,1,0:T(8,128)S(1)}, bf16[16,8,16,128]{3,2,1,0:T(8,128)(2,1)S(1)}, f32[1,32]{1,0:T(1,128)S(1)}) custom-call(f32[16,8,16,128]{3,2,1,0:T(8,128)} %n_hbm.1, f32[8,16,128]{2,1,0:T(8,128)} %p_hbm.1, f32[8,16,128]{2,1,0:T(8,128)} %t_hbm.1, s32[8,16,128]{2,1,0:T(8,128)} %flag_hbm.1, f32[8,16,128]{2,1,0:T(8,128)} %k_hbm.1, ...), custom_call_target="tpu_custom_call" | custom-call | tf_op jit(solution)/shard_map/newton_residual/pallas_call | solution.py:639
  22.9 1.2 %put_outputs.1 = (f32[16,8,16,128]{3,2,1,0:T(8,128)}, bf16[16,8,16,128]{3,2,1,0:T(8,128)(2,1)}, f32[1,32]{1,0:T(1,128)}) custom-call(f32[16,8,16,128]{3,2,1,0:T(8,128)S(1)} %get-tuple-element.6.resid, bf16[16,8,16,128]{3,2,1,0:T(8,128)(2,1)S(1)} %get-tuple-element.7.lnphi, f32[1,32]{1,0:T(1,128)S(1)} %get-tuple-element.8.well), custom_call_target="tpu_custom_call" | custom-call | tf_op jit(solution)/shard_map/put_outputs/pallas_call | solution.py:657

commit v4 on v3

--- a/solution.py
+++ b/solution.py
@@ -85,8 +85,8 @@
 ):
     small_hbm, refs = refs[:SMALL], refs[SMALL:]
     exit_p, friction, *refs = refs
-    resid_ref, lnphi_ref, well_ref = refs[:3]
-    small_refs, refs = refs[3 : 3 + SMALL], refs[3 + SMALL :]
+    resid_ref, lnphi_ref, well_ref, st, wp_v, gin_v, inj_t = refs[:7]
+    small_refs, refs = refs[7 : 7 + SMALL], refs[7 + SMALL :]
     (
         trans,
         visc,
@@ -110,7 +110,6 @@
         flag_v,
         pore_v,
         old_v,
-        st,
         up_v,
         w_v,
         mob_v,
@@ -124,12 +123,9 @@
         a_v,
         b_v,
         z_v,
-        wp_v,
-        wn_v,
         c0_t,
         c1_t,
         cb_t,
-        inj_t,
         row_v,
         mail_out,
         mail_in,
@@ -315,15 +311,15 @@
         ).start()
         return 0
 
-    def tell(j, _):
+    def post_lower(j, _):
+        post(j, 0)
         pl.semaphore_signal(
             ready.at[line], inc=1, device_id={"sub": j}, device_id_type=MESH
         )
         return 0
 
     pl.semaphore_wait(barrier, expected)
-    lax.fori_loop(0, s, post, 0)
-    lax.fori_loop(0, s, tell, 0)
+    lax.fori_loop(0, s, post_lower, 0)
     mail = pltpu.make_async_remote_copy(
         src_ref=mail_out.at[pl.ds(0, n_sub - 1)],
         dst_ref=mail_in.at[pl.ds(0, n_sub - 1)],
@@ -518,32 +514,33 @@
         found = mm_nt(row_hot_b, part)
         dense = found if dense is None else dense + found
     wp_v[...] = dense[:, :LANES].reshape(CX, CY, LANES)
-    wn_v[...] = dense[:, LANES:].reshape(CX, CY, LANES)
-
-    mine = jnp.sum(table, axis=0, keepdims=True)
-    row_v[...] = jnp.broadcast_to(mine, tile)
+    gin_v[...] = mob_v[...] * dense[:, LANES:].reshape(CX, CY, LANES)
+
+    inflow = jnp.sum(table, axis=0, keepdims=True)
+    row_v[...] = jnp.broadcast_to(inflow, tile)
     rate = row_v[:, 32:64] - (cpp - 1.0) * row_v[:, 0:32]
     running = mm_full(rate, before_hot)
     well = base - friction[0] * running * jnp.abs(running)
     well_ref[...] = well[0:1]
 
-    def perforated(x, _):
-        wp, gain = wp_v[x], mob_v[x] * wn_v[x]
+
+def put(resid, lnphi, well, st, wp, gin, inj, resid_out, lnphi_out, well_out, done, sem):
+    others = [
+        pltpu.make_async_copy(lnphi, lnphi_out, sem.at[CX]),
+        pltpu.make_async_copy(well, well_out, sem.at[CX + 1]),
+    ]
+    for copy in others:
+        copy.start()
+    planes = []
+    for x in range(CX):
         for i in range(NC):
-            v = inj_t[i]
-            inj = jnp.concatenate([v, v], axis=0)
-            resid_ref[i, x] = resid_ref[i, x] + (st[i, x + 1, rows, :] * wp + gain * inj)
-        return 0
-
-    lax.fori_loop(0, CX, perforated, 0)
-
-
-def put(resid, lnphi, well, resid_out, lnphi_out, well_out, sem):
-    pairs = ((resid, resid_out), (lnphi, lnphi_out), (well, well_out))
-    copies = [pltpu.make_async_copy(a, b, sem.at[i]) for i, (a, b) in enumerate(pairs)]
-    for copy in copies:
-        copy.start()
-    for copy in copies:
+            v = inj[i]
+            into = gin[x] * jnp.concatenate([v, v], axis=0)
+            out = st[i, x + 1, pl.ds(8, CY), :] * wp[x]
+            done[i, x] = resid[i, x] + (out + into)
+        planes.append(pltpu.make_async_copy(done.at[:, x], resid_out.at[:, x], sem.at[x]))
+        planes[-1].start()
+    for copy in planes + others:
         copy.wait()
 
 
@@ -589,11 +586,9 @@
         pltpu.VMEM(field, jnp.int32),
         pltpu.VMEM(field, F32),
         pltpu.VMEM(every, F32),
-        pltpu.VMEM((NC + 2, CX + 2, CY + 16, LANES), F32),
         pltpu.VMEM(every, F32),
         pltpu.VMEM(every, F32),
-        *[pltpu.VMEM(field, F32) for _ in range(13)],
-        table,
+        *[pltpu.VMEM(field, F32) for _ in range(11)],
         table,
         table,
         table,
@@ -638,9 +633,15 @@
     )
     found = pl.pallas_call(
         functools.partial(body, n_grp, n_sub),
-        out_shape=outs,
+        out_shape=(
+            *outs,
+            jax.ShapeDtypeStruct((NC + 2, CX + 2, CY + 16, LANES), F32),
+            jax.ShapeDtypeStruct(field, F32),
+            jax.ShapeDtypeStruct(field, F32),
+            jax.ShapeDtypeStruct((NC, 8, LANES), F32),
+        ),
         in_specs=[hbm] * (7 + SMALL) + [smem] * 2,
-        out_specs=(vmem, vmem, vmem),
+        out_specs=(vmem,) * 7,
         scratch_shapes=held + scratch,
         compiler_params=pltpu.CompilerParams(
             collective_id=0, has_side_effects=True, vmem_limit_bytes=40 * 1024 * 1024
@@ -657,10 +658,10 @@
     return pl.pallas_call(
         put,
         out_shape=outs,
-        in_specs=[vmem] * 3,
+        in_specs=[vmem] * 7,
         out_specs=(hbm,) * 3,
-        scratch_shapes=[pltpu.SemaphoreType.DMA((3,))],
-        compiler_params=pltpu.CompilerParams(vmem_limit_bytes=4 * 1024 * 1024),
+        scratch_shapes=[pltpu.VMEM(every, F32), pltpu.SemaphoreType.DMA((CX + 2,))],
+        compiler_params=pltpu.CompilerParams(vmem_limit_bytes=8 * 1024 * 1024),
         name="put_outputs",
     )(*found)
 

time: 24.3 us -> 23.7 us (0.975)
  Pallas kernels: 22.2 us -> 21.6 us
    pallas_call x2, Pallas kernels: 22.2 us -> 21.6 us  [the longest x1 20.4 us: per_device(): pl.pallas_call(functools.partial(body, n_grp, n_sub), out_shape=(*outs, j...]
where the time goes in v4:
time: 23.7 us; the launch traced here: 23.5 us
  Pallas kernels  21.6 us (91%)
  between operations  1.94 us (8%)
    pallas_call x1, Pallas kernels, per_device(): pl.pallas_call(functools.partial(body, n_grp, n_sub), out_shape=(*outs, j...  20.4 us
    pallas_call x1, Pallas kernels, per_device(): pl.pallas_call(put, out_shape=outs, in_specs=[vmem] * 7, out_specs=(hbm,)...  1.23 us

profile of v4, /device:TPU:1, one launch (start us, length us, event | category | flops | bytes accessed | tf_op | source)
XLA Modules:
  0.0 23.5 jit_solution(14375558683439197371)
XLA Ops:
  1.9 20.4 %newton_residual.1 = (f32[16,8,16,128]{3,2,1,0:T(8,128)S(1)}, bf16[16,8,16,128]{3,2,1,0:T(8,128)(2,1)S(1)}, f32[1,32]{1,0:T(1,128)S(1)}, f32[18,10,32,128]{3,2,1...) custom-call(f32[16,8,16,128]{3,2,1,0:T(8,128)} %n_hbm.1, ...), custom_call_target="tpu_custom_call" | custom-call | tf_op jit(solution)/shard_map/newton_residual/pallas_call | solution.py:634
  22.3 1.2 %put_outputs.1 = (f32[16,8,16,128]{3,2,1,0:T(8,128)}, bf16[16,8,16,128]{3,2,1,0:T(8,128)(2,1)}, f32[1,32]{1,0:T(1,128)}) custom-call(f32[16,8,16,128]{3,2,1,0:T(8,128)S(1)} %get-tuple-element.10.resid, bf16[16,8,16,128]{3,2,1,0:T(8,128)(2,1)S(1)} %get-tuple-element.11.lnphi, f32[1,32]{1,0:T(1,128)S(1)} %get-tuple-element.12.well, ...), custom_call_target="tpu_custom_call" | custom-call | tf_op jit(solution)/shard_map/put_outputs/pallas_call | solution.py:658

commit v5 on v4

--- a/solution.py
+++ b/solution.py
@@ -168,7 +168,7 @@
         pltpu.make_async_copy(src, dst, small_sem.at[i])
         for i, (src, dst) in enumerate(zip(small_hbm, small_refs))
     ]
-    for load in small_loads + loads[:4]:
+    for load in small_loads[:SCALARS] + loads[:4]:
         load.start()
 
     barrier = pltpu.get_barrier_semaphore()
@@ -192,10 +192,10 @@
         + has_g_up.astype(jnp.int32)
         + has_g_down.astype(jnp.int32)
     )
-    for load in loads[4:]:
+    for load in small_loads[SCALARS:] + loads[4:]:
         load.start()
 
-    for load in small_loads:
+    for load in small_loads[:SCALARS]:
         load.wait()
 
     tile = (8, LANES)
@@ -205,27 +205,6 @@
         c0_t[i] = amount * (1.0 + slope)
         c1_t[i] = amount * slope / jnp.sqrt(jnp.full(tile, crit[i], F32))
         cb_t[i] = jnp.full(tile, covol[i], F32)
-
-    row_v[...] = jnp.zeros(tile, F32)
-    row_v[0:1, 64:96] = cpp_ref[...] - 1.0
-    own_row = row_v[0:1, :]
-
-    loc = [loc_ref[h : h + 1, :] for h in range(2)]
-    row_of = jnp.concatenate([v // LANES for v in loc], axis=1)
-    lane_of = jnp.concatenate([v % LANES for v in loc], axis=1)
-    member = jnp.concatenate([mem_ref[h : h + 1, :] for h in range(2)], axis=1)
-    segment = jnp.concatenate([seg_ref[h : h + 1, :] for h in range(2)], axis=1)
-    strength = jnp.concatenate([wi_ref[h : h + 1, :] for h in range(2)], axis=1)
-    wells = n_sub
-    place = jnp.where(iota((wells, wells), 0) == gmp_ref[...], 1.0, 0.0).astype(BF16)
-    slot_hot = mm(place, hot(member, wells).astype(BF16))
-    lane_hot = hot(lane_of, LANES)
-    lane_hot_b = lane_hot.astype(BF16)
-    row_mask = iota((LANES, 2 * LANES), 0) == row_of
-    row_hot_b = jnp.where(row_mask, 1.0, 0.0).astype(BF16)
-    seg_hot = hot(segment, LANES).astype(BF16)
-    seg_hot_2 = hot(segment + 32, LANES).astype(BF16)
-    seg_hot_3 = hot(segment + 64, LANES).astype(BF16)
 
     def wide(table, i):
         v = table[i]
@@ -271,7 +250,31 @@
 
     lax.fori_loop(0, 2, phase, 0)
 
+    for load in small_loads[SCALARS:]:
+        load.wait()
     loads[4].wait()
+
+    row_v[...] = jnp.zeros(tile, F32)
+    row_v[0:1, 64:96] = cpp_ref[...] - 1.0
+    own_row = row_v[0:1, :]
+
+    loc = [loc_ref[h : h + 1, :] for h in range(2)]
+    row_of = jnp.concatenate([v // LANES for v in loc], axis=1)
+    lane_of = jnp.concatenate([v % LANES for v in loc], axis=1)
+    member = jnp.concatenate([mem_ref[h : h + 1, :] for h in range(2)], axis=1)
+    segment = jnp.concatenate([seg_ref[h : h + 1, :] for h in range(2)], axis=1)
+    strength = jnp.concatenate([wi_ref[h : h + 1, :] for h in range(2)], axis=1)
+    wells = n_sub
+    place = jnp.where(iota((wells, wells), 0) == gmp_ref[...], 1.0, 0.0).astype(BF16)
+    slot_hot = mm(place, hot(member, wells).astype(BF16))
+    lane_hot = hot(lane_of, LANES)
+    lane_hot_b = lane_hot.astype(BF16)
+    row_mask = iota((LANES, 2 * LANES), 0) == row_of
+    row_hot_b = jnp.where(row_mask, 1.0, 0.0).astype(BF16)
+    seg_hot = hot(segment, LANES).astype(BF16)
+    seg_hot_2 = hot(segment + 32, LANES).astype(BF16)
+    seg_hot_3 = hot(segment + 64, LANES).astype(BF16)
+
     big_a, big_b = a_v[...], b_v[...]
     liquid = flag_v[...] == 1
     zed = jnp.where(liquid, big_b + 0.01, 1.0 + big_b)
@@ -328,78 +331,6 @@
         device_id=g_up,
         device_id_type=MESH,
     )
-
-    def carry(x, _):
-        share = mob_v[x] * inv_v[x]
-        for i in range(NC):
-            st[i, x + 1, rows, :] = n_v[i, x] * share
-        return 0
-
-    lax.fori_loop(0, CX, carry, 0)
-    loads[5].wait()
-
-    def gather_rows(c, _):
-        ys_lo[c] = st[c, inner, 8, :]
-        ys_hi[c] = st[c, inner, 8 + CY - 1, :]
-        return 0
-
-    lax.fori_loop(0, NC + 2, gather_rows, 0)
-
-    def halo_copy(src, dst, slot, peer):
-        return pltpu.make_async_remote_copy(
-            src_ref=src,
-            dst_ref=dst,
-            send_sem=halo_send.at[slot],
-            recv_sem=halo_recv.at[slot],
-            device_id=peer,
-            device_id_type=MESH,
-        )
-
-    halo_copies = [
-        halo_copy(st.at[:, CX, rows], st.at[:, 0, rows], 0, g_up),
-        halo_copy(st.at[:, 1, rows], st.at[:, CX + 1, rows], 1, g_down),
-        halo_copy(ys_hi, yr_lo, 2, s_up),
-        halo_copy(ys_lo, yr_hi, 3, s_down),
-    ]
-    sends = (has_g_up, has_g_down, has_s_up, has_s_down)
-    receives = (has_g_down, has_g_up, has_s_down, has_s_up)
-
-    for there, copy in zip(sends, halo_copies):
-        pl.when(there)(copy.start)
-
-    @pl.when(jnp.logical_not(has_g_down))
-    def _():
-        st[:, 0, rows, :] = jnp.zeros((NC + 2, CY, LANES), F32)
-
-    @pl.when(jnp.logical_not(has_g_up))
-    def _():
-        st[:, CX + 1, rows, :] = jnp.zeros((NC + 2, CY, LANES), F32)
-
-    @pl.when(jnp.logical_not(has_s_down))
-    def _():
-        yr_lo[...] = jnp.zeros((NC + 2, CX, LANES), F32)
-
-    @pl.when(jnp.logical_not(has_s_up))
-    def _():
-        yr_hi[...] = jnp.zeros((NC + 2, CX, LANES), F32)
-
-    total = jnp.zeros(tile, F32)
-    for i in range(NC):
-        total = total + recipe[i]
-    for i in range(NC):
-        inj_t[i] = jnp.full(tile, recipe[i], F32) / total
-
-    order = jnp.where(iota((32, 32), 0) == order_ref[...], 1.0, 0.0).astype(F32)
-    sub32, lane32 = iota((32, 32), 0), iota((32, 32), 1)
-    upper = jnp.where(sub32 <= lane32, 1.0, 0.0).astype(F32)
-    after = jnp.where(sub32 == lane32 + 1, 1.0, 0.0).astype(F32)
-    before_hot = mm_full_nt(mm_full(order, upper), order)
-    next_hot = mm_full_nt(mm_full(order, after), order)
-    last_row = jnp.where(iota((8, 32), 1) == 31, 1.0, 0.0).astype(F32)
-    last_hot = mm_full_nt(last_row, order)
-    cpp = jnp.broadcast_to(cpp_ref[...], (8, 32))
-    base = cpp - (mm_full(cpp, next_hot) + exit_p[0] * last_hot)
-
 
     loads[6].wait()
 
@@ -425,6 +356,78 @@
         return 0
 
     lax.fori_loop(0, 2, fugacity, 0)
+
+    def carry(x, _):
+        share = mob_v[x] * inv_v[x]
+        for i in range(NC):
+            st[i, x + 1, rows, :] = n_v[i, x] * share
+        return 0
+
+    lax.fori_loop(0, CX, carry, 0)
+    loads[5].wait()
+
+    def gather_rows(c, _):
+        ys_lo[c] = st[c, inner, 8, :]
+        ys_hi[c] = st[c, inner, 8 + CY - 1, :]
+        return 0
+
+    lax.fori_loop(0, NC + 2, gather_rows, 0)
+
+    def halo_copy(src, dst, slot, peer):
+        return pltpu.make_async_remote_copy(
+            src_ref=src,
+            dst_ref=dst,
+            send_sem=halo_send.at[slot],
+            recv_sem=halo_recv.at[slot],
+            device_id=peer,
+            device_id_type=MESH,
+        )
+
+    halo_copies = [
+        halo_copy(st.at[:, CX, rows], st.at[:, 0, rows], 0, g_up),
+        halo_copy(st.at[:, 1, rows], st.at[:, CX + 1, rows], 1, g_down),
+        halo_copy(ys_hi, yr_lo, 2, s_up),
+        halo_copy(ys_lo, yr_hi, 3, s_down),
+    ]
+    sends = (has_g_up, has_g_down, has_s_up, has_s_down)
+    receives = (has_g_down, has_g_up, has_s_down, has_s_up)
+
+    for there, copy in zip(sends, halo_copies):
+        pl.when(there)(copy.start)
+
+    @pl.when(jnp.logical_not(has_g_down))
+    def _():
+        st[:, 0, rows, :] = jnp.zeros((NC + 2, CY, LANES), F32)
+
+    @pl.when(jnp.logical_not(has_g_up))
+    def _():
+        st[:, CX + 1, rows, :] = jnp.zeros((NC + 2, CY, LANES), F32)
+
+    @pl.when(jnp.logical_not(has_s_down))
+    def _():
+        yr_lo[...] = jnp.zeros((NC + 2, CX, LANES), F32)
+
+    @pl.when(jnp.logical_not(has_s_up))
+    def _():
+        yr_hi[...] = jnp.zeros((NC + 2, CX, LANES), F32)
+
+    total = jnp.zeros(tile, F32)
+    for i in range(NC):
+        total = total + recipe[i]
+    for i in range(NC):
+        inj_t[i] = jnp.full(tile, recipe[i], F32) / total
+
+    order = jnp.where(iota((32, 32), 0) == order_ref[...], 1.0, 0.0).astype(F32)
+    sub32, lane32 = iota((32, 32), 0), iota((32, 32), 1)
+    upper = jnp.where(sub32 <= lane32, 1.0, 0.0).astype(F32)
+    after = jnp.where(sub32 == lane32 + 1, 1.0, 0.0).astype(F32)
+    before_hot = mm_full_nt(mm_full(order, upper), order)
+    next_hot = mm_full_nt(mm_full(order, after), order)
+    last_row = jnp.where(iota((8, 32), 1) == 31, 1.0, 0.0).astype(F32)
+    last_hot = mm_full_nt(last_row, order)
+    cpp = jnp.broadcast_to(cpp_ref[...], (8, 32))
+    base = cpp - (mm_full(cpp, next_hot) + exit_p[0] * last_hot)
+
 
     for there, copy in zip(receives, halo_copies):
         pl.when(there)(copy.wait_recv)

time: 23.7 us -> 23.7 us (level)
  no operation moved by 1% of the time
where the time goes in v5:
time: 23.7 us; the launch traced here: 23.5 us
  Pallas kernels  21.5 us (91%)
  between operations  1.94 us (8%)
    pallas_call x1, Pallas kernels, per_device(): pl.pallas_call(functools.partial(body, n_grp, n_sub), out_shape=(*outs, j...  20.3 us
    pallas_call x1, Pallas kernels, per_device(): pl.pallas_call(put, out_shape=outs, in_specs=[vmem] * 7, out_specs=(hbm,)...  1.23 us

profile of v5, /device:TPU:1, one launch (start us, length us, event | category | flops | bytes accessed | tf_op | source)
XLA Modules:
  0.0 23.5 jit_solution(10293284274856146731)
XLA Ops:
  1.9 20.3 %newton_residual.1 = (f32[16,8,16,128]{3,2,1,0:T(8,128)S(1)}, bf16[16,8,16,128]{3,2,1,0:T(8,128)(2,1)S(1)}, f32[1,32]{1,0:T(1,128)S(1)}, f32[18,10,32,128]{3,2,1...) custom-call(f32[16,8,16,128]{3,2,1,0:T(8,128)} %n_hbm.1, ...), custom_call_target="tpu_custom_call" | custom-call | tf_op jit(solution)/shard_map/newton_residual/pallas_call | solution.py:637
  22.2 1.2 %put_outputs.1 = (f32[16,8,16,128]{3,2,1,0:T(8,128)}, bf16[16,8,16,128]{3,2,1,0:T(8,128)(2,1)}, f32[1,32]{1,0:T(1,128)}) custom-call(f32[16,8,16,128]{3,2,1,0:T(8,128)S(1)} %get-tuple-element.10.resid, bf16[16,8,16,128]{3,2,1,0:T(8,128)(2,1)S(1)} %get-tuple-element.11.lnphi, f32[1,32]{1,0:T(1,128)S(1)} %get-tuple-element.12.well, ...), custom_call_target="tpu_custom_call" | custom-call | tf_op jit(solution)/shard_map/put_outputs/pallas_call | solution.py:661
